TPU v7x, 768 devices: a whole 4x8x12 slice. The times are simulated.
768 devices in a mesh: dp: 48 (over x_lo, z, core), tp: 16 (over x_hi, y).
Axes of the slice: x: 4 (x_hi: 2, x_lo: 2; x = x_hi * 2 + x_lo), y: 8, z: 12, core: 2. Of those that a mesh axis runs over, the one named last changes fastest.
Arguments:
- student_hidden: bfloat16 [6912, 3456], P('dp'), may hold values from -6 to 6
- norm_gain: float32 [3456], replicated, may hold values from 0.25 to 1.75
- projection: bfloat16 [3456, 8192], P(None, 'tp'), may hold values from -0.109375 to 0.109375
- teacher_partials: bfloat16 [16, 6912, 8192], P('tp', 'dp'), may hold values from -5 to 5
- teacher_residual: bfloat16 [6912, 8192], P('dp', 'tp'), may hold values from -90 to 90
- owner: int32 [6912], P('dp'), may hold values from 0 to 6911, as said below
Outputs:
- grad_scaled: float32 [3456, 8192], P('dp', 'tp')
Inputs may be any that keep to these rules, and one draw needn't show every extreme that they name: owner is a permutation of all token indices; the 144 teacher rows of each index of dp hold exactly 3 tokens owned by each index of dp.
All inputs are finite; a program needn't handle non-finite values.
Results may differ from a plain program's by a relative error of at most 0.009.
Values may be sent and summed in bfloat16 or wider, within the bound.
No kernel may reach another device: no remote copies, remote signals or barrier semaphores. Data moves between devices by JAX's collectives and lax.ppermute only.
A program may use at most 64 MiB of HBM per device.

v0:
```python
import functools

import jax
import jax.numpy as jnp
from jax import lax
from jax.sharding import Mesh
from jax.sharding import PartitionSpec as P

DP_TP = ("dp_0", "dp_1", "dp_2", "tp_0", "tp_1")
TP = ("tp_0", "tp_1")
DP = ("dp_0", "dp_1", "dp_2")


def one_axis_at_a_time(array, axes):
    return functools.reduce(lax.pmax, axes, array)


def sum_in_order(tiles, axes, order):
    lengths = [lax.axis_size(a) for a in axes]
    tiles = tiles.reshape(*lengths, *tiles.shape[1:])
    tiles = tiles.transpose(*order, *range(len(axes), tiles.ndim))
    tiles = tiles.reshape(-1, *tiles.shape[len(axes) :])
    for k in order:
        tiles = lax.psum_scatter(tiles, axes[k], scatter_dimension=0, tiled=True)
    return tiles[0]


def in_blocks(array, dim, peers):
    lengths = array.shape
    tiles = array.reshape(*lengths[:dim], peers, lengths[dim] // peers, *lengths[dim + 1 :])
    return jnp.moveaxis(tiles, dim, 0)


def summed_rows(array, axes, order, dim):
    peers = lax.axis_size(axes)
    return sum_in_order(in_blocks(array, dim, peers), axes, order)


def agree(largest):
    return one_axis_at_a_time(largest, DP_TP) + 1e-06


def rounded_terms(partial_value, scale):
    return lax.optimization_barrier((partial_value / scale).astype(jnp.bfloat16)).astype(
        jnp.float32
    )


def per_device(student_hidden, norm_gain, projection, teacher_partials, teacher_residual, owner):
    columns = projection.shape[1]
    rows_dev = student_hidden.shape[0]
    terms_in = teacher_partials[0].astype(jnp.float32)
    summed = summed_rows(terms_in.astype(jnp.bfloat16), TP, (1, 0), 1).astype(jnp.float32)
    teacher = (teacher_residual.astype(jnp.float32) + summed).astype(jnp.bfloat16)
    groups = lax.axis_size(DP)
    slots = rows_dev // groups
    destination = owner // rows_dev
    order = jnp.argsort(destination, stable=True)
    outgoing = teacher[order].reshape(groups, slots, columns)
    outgoing_owner = owner[order].reshape(groups, slots)
    arrived, arrived_owner = (
        lax.all_to_all(outgoing, DP, split_axis=0, concat_axis=0, tiled=True),
        lax.all_to_all(outgoing_owner, DP, split_axis=0, concat_axis=0, tiled=True),
    )
    placing = jnp.argsort(arrived_owner.reshape(-1) % rows_dev)
    target = arrived.reshape(rows_dev, columns)[placing]
    values = student_hidden.astype(jnp.float32)
    inverse = lax.rsqrt(jnp.mean(values * values, axis=-1, keepdims=True) + 1e-05)
    normed = (values * inverse * norm_gain).astype(jnp.bfloat16)
    pred = jnp.dot(normed, projection, preferred_element_type=jnp.float32)
    diff = (pred - target.astype(jnp.float32)).astype(jnp.bfloat16)
    partial_value = lax.dot_general(
        normed, diff, (((0,), (0,)), ((), ())), preferred_element_type=jnp.float32
    )
    scale = agree(jnp.max(jnp.abs(partial_value)))
    grad_scaled = summed_rows(rounded_terms(partial_value, scale), DP, (2, 1, 0), 0)
    return grad_scaled


def solution(mesh):
    torus = Mesh(mesh.devices.reshape(2, 12, 2, 2, 8), ("dp_0", "dp_1", "dp_2", "tp_0", "tp_1"))
    placed = (P(DP, None), P(), P(None, TP), P(TP, DP, None), P(DP, TP), P(DP))
    return jax.shard_map(
        per_device, mesh=torus, in_specs=placed, out_specs=P(DP, TP), check_vma=False
    )
```

profile of v0, /device:TPU:1, one launch (start us, length us, event | category | flops | bytes accessed | tf_op | source)
XLA Modules:
  0.0 322.9 jit_solution(15035721984367842452)
XLA Ops:
  6.5 0.0 copy-start
  6.5 0.0 reduce-scatter.6.cloned.1.call-start
  6.5 2.8 copy.18
  9.3 0.0 copy-start.1
  9.3 2.7 copy.14
  12.1 0.0 reduce-scatter.6.cloned.1.call-update
  12.1 0.0 reduce-scatter.8.cloned.1.call-start
  12.1 0.0 copy-done.1
  12.2 3.2 sort.34
  15.3 49.1 %reduce-scatter.6.cloned.1.call-done = bf16[2,144,512]{2,1,0:T(8,128)(2,1)} async-done(((bf16[16,144,512]{2,1,0:T(8,128)(2,1)}), bf16[2,144,512]{2,1,0:T(8,128)(2,1)}) %reduce-scatter.6.cloned.1.call-update) | async-done | bytes 294928 | tf_op jit(solution)/shard_map/reduce_scatter | solution.py:24
  64.5 0.0 reduce-scatter.8.cloned.1.call-update
  64.5 1.6 gather_fusion.1
  66.1 0.7 all_to_all.10
  66.9 15.8 %all-to-all-start.1 = ((s32[48,1,3]{2,1,0:T(1,128)}), s32[48,1,3]{2,1,0:T(1,128)}, u32[]{:S(2)}, u32[]{:S(2)}) async-start(s32[48,1,3]{2,1,0:T(1,128)} %bitcast.26), calls=%async_computation.3 | async-start | bytes 49152 | tf_op jit(solution)/shard_map/all_to_all | solution.py:63
  82.7 1.5 fusion
  84.2 8.7 %all-to-all-done.1 = s32[48,1,3]{2,1,0:T(1,128)} async-done(((s32[48,1,3]{2,1,0:T(1,128)}), s32[48,1,3]{2,1,0:T(1,128)}, u32[]{:S(2)}, u32[]{:S(2)}) %all-to-all-start.1) | async-done | bytes 608 | tf_op jit(solution)/shard_map/all_to_all | solution.py:63
  92.9 1.5 remainder_reduce_fusion
  94.3 0.9 rem.23
  95.2 0.0 reduce-scatter.8.cloned.1.call-done
  95.2 1.7 fusion.11
  96.9 2.5 gather_fusion
  99.4 1.7 reshape.44
  101.1 11.1 %all-to-all-start = ((bf16[48,3,512]{2,1,0:T(4,128)(2,1)}), bf16[48,3,512]{2,1,0:T(4,128)(2,1)}, u32[]{:S(2)}, u32[]{:S(2)}) async-start(bf16[48,3,512]{2,1,0:T(4,128)(2,1)} %reshape.44), calls=%async_computation.2 | async-start | bytes 393216 | tf_op jit(solution)/shard_map/all_to_all | solution.py:62
  112.2 0.0 reduce-scatter.10.cloned.1.call-start
  112.2 3.2 sort.35
  115.4 10.4 %all-to-all-done = bf16[48,3,512]{2,1,0:T(4,128)(2,1)} async-done(((bf16[48,3,512]{2,1,0:T(4,128)(2,1)}), bf16[48,3,512]{2,1,0:T(4,128)(2,1)}, u32[]{:S(2)}, u32[]{:S(2)}) %all-to-all-start) | async-done | bytes 147488 | tf_op jit(solution)/shard_map/all_to_all | solution.py:62
  125.8 1.7 reshape.45
  127.6 2.5 gather_fusion.2
  130.1 0.0 copy-done
  130.1 6.9 %abs_reduce_fusion = (f32[]{:T(128)}, f32[3456,512]{1,0:T(8,128)}) fusion(bf16[3456,512]{1,0:T(8,128)(2,1)S(1)} %copy-done, bf16[144,3456]{1,0:T(8,128)(2,1)} %param.6, f32[3456]{0:T(1024)} %param.7, f32[144]{0:T(256)S(1)} %add_rsqrt_fusion, bf16[144,512]{1,0:T(8,128)(2,1)} %gather_fusion.2), kind=kOutput, calls=%fused_computation.5 | convolution fusion | flops 1026957312 | bytes 11774020 | tf_op jit(solution)/shard_map/dot_general | solution.py:72
  137.0 4.4 %pmax.35 = f32[]{:T(128)} all-reduce(f32[]{:T(128)} %get-tuple-element.9), channel_id=1, replica_groups=mesh['dp_0'=2,'dp_1'=12,'dp_2'=2,'tp_0'=2,'tp_1'=8] {'dp_0'}, use_global_device_ids=true, to_apply=%region_6.7 | all-reduce | flops 1 | bytes 8 | tf_op jit(solution)/shard_map/pmax | solution.py:15
  141.4 16.6 %pmax.36 = f32[]{:T(128)} all-reduce(f32[]{:T(128)} %pmax.35), channel_id=1, replica_groups=mesh['dp_0'=2,'dp_1'=12,'dp_2'=2,'tp_0'=2,'tp_1'=8] {'dp_1'}, use_global_device_ids=true, to_apply=%region_7.8 | all-reduce | flops 1 | bytes 8 | tf_op jit(solution)/shard_map/pmax | solution.py:15
  158.0 10.4 %pmax.37 = f32[]{:T(128)} all-reduce(f32[]{:T(128)} %pmax.36), channel_id=1, replica_groups=mesh['dp_0'=2,'dp_1'=12,'dp_2'=2,'tp_0'=2,'tp_1'=8] {'dp_2'}, use_global_device_ids=true, to_apply=%region_8.9 | all-reduce | flops 1 | bytes 8 | tf_op jit(solution)/shard_map/pmax | solution.py:15
  168.4 5.9 %pmax.38 = f32[]{:T(128)} all-reduce(f32[]{:T(128)} %pmax.37), channel_id=1, replica_groups=mesh['dp_0'=2,'dp_1'=12,'dp_2'=2,'tp_0'=2,'tp_1'=8] {'tp_0'}, use_global_device_ids=true, to_apply=%region_9.10 | all-reduce | flops 1 | bytes 8 | tf_op jit(solution)/shard_map/pmax | solution.py:15
  174.3 13.8 %pmax.39 = f32[]{:T(128)} all-reduce(f32[]{:T(128)} %pmax.38), channel_id=1, replica_groups=mesh['dp_0'=2,'dp_1'=12,'dp_2'=2,'tp_0'=2,'tp_1'=8] {'tp_1'}, use_global_device_ids=true, to_apply=%region_10.11 | all-reduce | flops 1 | bytes 8 | tf_op jit(solution)/shard_map/pmax | solution.py:15
  188.8 4.0 %divide_convert_fusion = bf16[3456,512]{1,0:T(8,128)(2,1)S(1)} fusion(f32[3456,512]{1,0:T(8,128)} %get-tuple-element.10, f32[]{:T(128)S(6)} %add.47), kind=kLoop, calls=%fused_computation.4 | loop fusion | flops 3538944 | bytes 10616836 | tf_op jit(solution)/shard_map/convert_element_type | solution.py:44
  192.8 1.0 convert_bitcast_fusion
  193.8 3.8 %copy.16 = f32[2,12,2,72,512]{4,3,2,1,0:T(8,128)} copy(f32[2,12,2,72,512]{4,3,0,1,2:T(8,128)S(1)} %convert_bitcast_fusion) | data formatting | bytes 14155776 | tf_op jit(solution)/shard_map/reshape | solution.py:22
  197.6 0.0 reduce-scatter.10.cloned.1.call-update
  197.6 0.0 reduce-scatter.12.cloned.1.call-start
  197.6 24.9 %reduce-scatter.10.cloned.1.call-done = f32[24,72,512]{2,1,0:T(8,128)} async-done(((f32[48,72,512]{2,1,0:T(8,128)}), f32[24,72,512]{2,1,0:T(8,128)}) %reduce-scatter.10.cloned.1.call-update) | async-done | bytes 3538960 | tf_op jit(solution)/shard_map/reduce_scatter | solution.py:24
  222.6 0.0 reduce-scatter.12.cloned.1.call-update
  222.6 0.0 reduce-scatter.14.cloned.1.call-start
  222.6 63.4 %reduce-scatter.12.cloned.1.call-done = f32[2,72,512]{2,1,0:T(8,128)} async-done(((f32[24,72,512]{2,1,0:T(8,128)}), f32[2,72,512]{2,1,0:T(8,128)}) %reduce-scatter.12.cloned.1.call-update) | async-done | bytes 294928 | tf_op jit(solution)/shard_map/reduce_scatter | solution.py:24
  286.1 0.0 reduce-scatter.14.cloned.1.call-update
  286.1 30.3 %reduce-scatter.14.cloned.1.call-done = f32[1,72,512]{2,1,0:T(8,128)} async-done(((f32[2,72,512]{2,1,0:T(8,128)}), f32[1,72,512]{2,1,0:T(8,128)}) %reduce-scatter.14.cloned.1.call-update) | async-done | bytes 147472 | tf_op jit(solution)/shard_map/reduce_scatter | solution.py:24
  (9 shorter events, 0.1 us)
Async XLA Ops:
  6.5 123.5 %copy-start = (bf16[3456,512]{1,0:T(8,128)(2,1)S(1)}, bf16[3456,512]{1,0:T(8,128)(2,1)}, u32[]{:S(2)}) copy-start(bf16[3456,512]{1,0:T(8,128)(2,1)} %param.8) | copy-start | bytes 10616836
  6.5 57.9 %reduce-scatter.6.cloned.1.call-start = ((), (), s32[]{:S(2)}) async-start(), calls=%async_computation.7 | async-start | bytes 2654208 | tf_op jit(solution)/shard_map/reduce_scatter | solution.py:24
  9.3 2.8 copy-start.1
  12.1 83.1 %reduce-scatter.8.cloned.1.call-start = ((), (), s32[]{:S(2)}) async-start(), calls=%async_computation.8 | async-start | bytes 442368 | tf_op jit(solution)/shard_map/reduce_scatter | solution.py:24
  66.9 26.0 %all-to-all-start.1 = ((s32[48,1,3]{2,1,0:T(1,128)}), s32[48,1,3]{2,1,0:T(1,128)}, u32[]{:S(2)}, u32[]{:S(2)}) async-start(s32[48,1,3]{2,1,0:T(1,128)} %bitcast.26), calls=%async_computation.3 | async-start | bytes 49152 | tf_op jit(solution)/shard_map/all_to_all | solution.py:63
  101.1 24.8 %all-to-all-start = ((bf16[48,3,512]{2,1,0:T(4,128)(2,1)}), bf16[48,3,512]{2,1,0:T(4,128)(2,1)}, u32[]{:S(2)}, u32[]{:S(2)}) async-start(bf16[48,3,512]{2,1,0:T(4,128)(2,1)} %reshape.44), calls=%async_computation.2 | async-start | bytes 393216 | tf_op jit(solution)/shard_map/all_to_all | solution.py:62
  112.2 110.4 %reduce-scatter.10.cloned.1.call-start = ((), (), s32[]{:S(2)}) async-start(), calls=%async_computation.9 | async-start | bytes 10616832 | tf_op jit(solution)/shard_map/reduce_scatter | solution.py:24
  197.6 88.5 %reduce-scatter.12.cloned.1.call-start = ((), (), s32[]{:S(2)}) async-start(), calls=%async_computation.10 | async-start | bytes 3833856 | tf_op jit(solution)/shard_map/reduce_scatter | solution.py:24
  222.6 93.8 %reduce-scatter.14.cloned.1.call-start = ((), (), s32[]{:S(2)}) async-start(), calls=%async_computation.11 | async-start | bytes 442368 | tf_op jit(solution)/shard_map/reduce_scatter | solution.py:24
Sparse Core Ops, SparseCore 0:
  12.2 52.2 reduce-scatter.5
  67.5 27.3 reduce-scatter.7
  197.7 24.7 reduce-scatter.9
  225.6 60.4 reduce-scatter.11
  289.0 27.4 reduce-scatter.13
where the time goes:
time: 324 us; the launch traced here: 323 us
  waiting for transfers between devices  187 us (58%)
  blocking collectives  51.1 us (16%)
  starting transfers between devices  27 us (8%)
  local copies, waits for them, and re-layouts  20.9 us (6%)
  other arithmetic  16 us (5%)
  between operations  13.9 us (4%)
  matrix products  6.95 us (2%)
    reduce_scatter x5, waiting for transfers between devices, sum_in_order(): tiles = lax.psum_scatter(tiles, axes[k], scatter_dimension=0, tiled=True)  168 us
    pmax x5, blocking collectives, one_axis_at_a_time(): return functools.reduce(lax.pmax, axes, array)  51.1 us
    all_to_all x1, starting transfers between devices, per_device(): lax.all_to_all(outgoing_owner, DP, split_axis=0, concat_axis=0, tiled=True)  15.8 us
    all_to_all x1, starting transfers between devices, per_device(): lax.all_to_all(outgoing, DP, split_axis=0, concat_axis=0, tiled=True)  11.1 us
    all_to_all x1, waiting for transfers between devices, per_device(): lax.all_to_all(outgoing, DP, split_axis=0, concat_axis=0, tiled=True)  10.4 us
    all_to_all x1, waiting for transfers between devices, per_device(): lax.all_to_all(outgoing_owner, DP, split_axis=0, concat_axis=0, tiled=True)  8.68 us
    dot_general x1, matrix products, per_device(): lax.dot_general(normed, diff, (((0,), (0,)), ((), ())), preferred_element...  6.95 us
  transfers between devices with their start and end apart: 7, of which 6 were waited for; matrix products, arithmetic and copies ran while one was open for 4% of the time, Pallas kernels for 0%

commit v1 on v0

v1 whole, which is shorter than its diff:
```python
import jax
import jax.numpy as jnp
from jax import lax
from jax.experimental import pallas as pl
from jax.experimental.pallas import tpu as pltpu
from jax.sharding import Mesh
from jax.sharding import PartitionSpec as P

X, Z, C = "dp_0", "dp_1", "dp_2"
XH, Y = "tp_0", "tp_1"
DP, TP, XC = (X, Z, C), (XH, Y), (X, C)
VMEM = pl.BlockSpec(memory_space=pltpu.VMEM)
SMEM = pl.BlockSpec(memory_space=pltpu.SMEM)
ROWS_FIRST = (((0,), (0,)), ((), ()))
MARKS = 128


def exchange(array, axes):
    return lax.all_to_all(array, axes, split_axis=0, concat_axis=0, tiled=True)


def to_peer(array, k):
    return lax.ppermute(array, XC, [(p, p ^ k) for p in range(4)])


def cost(flops, moved):
    return pl.CostEstimate(flops=flops, bytes_accessed=moved, transcendentals=0)


def split_kernel(in_ref, out_ref):
    out_ref[0] = in_ref[...]


def split_columns(array, parts):
    rows, width = array.shape
    columns = width // parts
    return pl.pallas_call(
        split_kernel,
        out_shape=jax.ShapeDtypeStruct((parts, rows, columns), array.dtype),
        grid=(parts,),
        in_specs=[pl.BlockSpec((rows, columns), lambda k: (0, k))],
        out_specs=pl.BlockSpec((1, rows, columns), lambda k: (k, 0, 0)),
        name="split_columns",
        cost_estimate=cost(0, 4 * rows * width),
    )(array)


def student_kernel(sizes, me_ref, hidden_ref, gain_ref, proj_ref, pred_ref, parts_ref, wide_ref, part_ref):
    nx, nz, nc, block = sizes
    values = hidden_ref[...].astype(jnp.float32)
    inverse = lax.rsqrt(jnp.mean(values * values, axis=-1, keepdims=True) + 1e-05)
    normed = values * inverse * gain_ref[...]
    pred = jnp.dot(normed.astype(jnp.bfloat16), proj_ref[...], preferred_element_type=jnp.float32)
    pred_ref[...] = pred.astype(jnp.bfloat16)
    wide_ref[...] = normed
    for p in range(nx * nc):
        x, c = p // nc, p % nc
        for z in range(nz):
            start = ((x * nz + z) * nc + c) * block
            part_ref[:, z * block : (z + 1) * block] = wide_ref[:, start : start + block]
        parts_ref[p ^ me_ref[0]] = part_ref[...].astype(jnp.bfloat16)


def student(me, hidden, gain, projection, sizes):
    nx, nz, nc, block = sizes
    rows, features = hidden.shape
    columns = projection.shape[1]
    return pl.pallas_call(
        lambda *refs: student_kernel(sizes, *refs),
        out_shape=(
            jax.ShapeDtypeStruct((rows, columns), jnp.bfloat16),
            jax.ShapeDtypeStruct((nx * nc, rows, nz * block), jnp.bfloat16),
        ),
        in_specs=[SMEM, VMEM, VMEM, VMEM],
        out_specs=(VMEM, VMEM),
        scratch_shapes=[
            pltpu.VMEM((rows, features), jnp.float32),
            pltpu.VMEM((rows, nz * block), jnp.float32),
        ],
        name="student",
        cost_estimate=cost(2 * rows * features * columns, 2 * features * columns),
    )(me, hidden, gain, projection)


def teacher_kernel(terms_ref, residual_ref, slot_ref, marks_ref, out_ref):
    count, rows, columns = terms_ref.shape
    summed = terms_ref[0].astype(jnp.float32)
    for k in range(1, count):
        summed = summed + terms_ref[k].astype(jnp.float32)
    teacher = (residual_ref[...].astype(jnp.float32) + summed).astype(jnp.bfloat16)
    lanes = lax.broadcasted_iota(jnp.int32, (rows, out_ref.shape[0]), 1)
    select = (lanes == slot_ref[...]).astype(jnp.float32).astype(jnp.bfloat16)
    for at, part in ((0, teacher), (columns, marks_ref[...])):
        moved = lax.dot_general(select, part, ROWS_FIRST, preferred_element_type=jnp.float32)
        out_ref[:, at : at + part.shape[1]] = moved.astype(jnp.bfloat16)


def teacher_rows(terms, residual, slot, marks, slots):
    rows, columns = residual.shape
    return pl.pallas_call(
        teacher_kernel,
        out_shape=jax.ShapeDtypeStruct((slots, columns + MARKS), jnp.bfloat16),
        in_specs=[VMEM] * 4,
        out_specs=VMEM,
        name="teacher_rows",
        cost_estimate=cost(2 * rows * columns * slots, 2 * terms.size),
    )(terms, residual, slot, marks)


def gradient_kernel(me_ref, rows_ref, pred_ref, normed_ref, sum_ref, max_ref):
    groups, per, height = normed_ref.shape
    columns = pred_ref.shape[-1]
    peer = rows_ref[:, columns : columns + 1].astype(jnp.float32).astype(jnp.int32)
    local = rows_ref[:, columns + 1 : columns + 2].astype(jnp.float32).astype(jnp.int32)
    place = (peer ^ me_ref[0]) * per + local
    lanes = lax.broadcasted_iota(jnp.int32, (rows_ref.shape[0], groups * per), 1)
    select = (lanes == place).astype(jnp.float32).astype(jnp.bfloat16)
    target = lax.dot_general(
        select, rows_ref[:, :columns], ROWS_FIRST, preferred_element_type=jnp.float32
    )
    largest = jnp.zeros((1, 1), jnp.float32)
    total = None
    for g in range(groups):
        aimed = target[g * per : (g + 1) * per]
        diff = (pred_ref[g].astype(jnp.float32) - aimed).astype(jnp.bfloat16)
        part = lax.dot_general(normed_ref[g], diff, ROWS_FIRST, preferred_element_type=jnp.float32)
        largest = jnp.maximum(largest, jnp.max(jnp.abs(part), keepdims=True))
        total = part if total is None else total + part
    sum_ref[...] = total.astype(jnp.bfloat16)
    max_ref[...] = jnp.broadcast_to(largest, max_ref.shape)


def gradient(me, rows, pred, normed):
    groups, per, height = normed.shape
    columns = pred.shape[-1]
    return pl.pallas_call(
        gradient_kernel,
        out_shape=(
            jax.ShapeDtypeStruct((height, columns), jnp.bfloat16),
            jax.ShapeDtypeStruct((8, 128), jnp.float32),
        ),
        in_specs=[SMEM, VMEM, VMEM, VMEM],
        out_specs=(VMEM, VMEM),
        name="gradient",
        cost_estimate=cost(4 * groups * per * height * columns, 4 * normed.size),
    )(me, rows, pred, normed)


def per_device(student_hidden, norm_gain, projection, teacher_partials, teacher_residual, owner):
    rows_dev, columns = teacher_residual.shape
    features = student_hidden.shape[1]
    nx, nz, nc = (lax.axis_size(a) for a in DP)
    peers = nx * nc
    block = features // (nx * nz * nc)
    per_z = rows_dev // nz
    slots_z = -(-per_z // 16) * 16
    me = lax.axis_index(X) * nc + lax.axis_index(C)
    me_ref = me.reshape(1).astype(jnp.int32)

    with jax.named_scope("terms"):
        terms = exchange(split_columns(teacher_partials[0], lax.axis_size(TP)), TP)

    with jax.named_scope("student"):
        sizes = (nx, nz, nc, block)
        pred, parts = student(me_ref, student_hidden, norm_gain[None], projection, sizes)
        pred_parts = [pred] + [to_peer(pred, k) for k in range(1, peers)]
        normed_parts = [parts[0]] + [to_peer(parts[k], k) for k in range(1, peers)]
        pred_all, normed_all = jnp.stack(pred_parts), jnp.stack(normed_parts)

    with jax.named_scope("places"):
        whose = owner // rows_dev
        z_to = (whose // nc) % nz
        peer_to = (whose // (nz * nc)) * nc + whose % nc
        index = jnp.arange(rows_dev)
        earlier = (z_to[None, :] == z_to[:, None]) & (index[None, :] < index[:, None])
        slot = z_to * slots_z + jnp.sum(earlier.astype(jnp.int32), axis=1)
        lane = lax.broadcasted_iota(jnp.int32, (rows_dev, MARKS), 1)
        marks = jnp.where(lane == 0, peer_to[:, None], (owner % rows_dev)[:, None])
        marks = jnp.where(lane < 2, marks, 0).astype(jnp.bfloat16)
        slot = slot[:, None]

    terms, pred_all, normed_all, slot, marks = lax.optimization_barrier(
        (terms, pred_all, normed_all, slot, marks)
    )

    with jax.named_scope("regroup"):
        outgoing = teacher_rows(terms, teacher_residual, slot, marks, nz * slots_z)
        arrived = exchange(outgoing.reshape(nz, slots_z, -1), Z).reshape(nz * slots_z, -1)
        rows = lax.all_gather(arrived, XC, axis=0, tiled=True)

    with jax.named_scope("grad"):
        tile, largest = gradient(me_ref, rows, pred_all, normed_all)
        pieces = exchange(tile.reshape(nz, block, columns), Z)
        scale = jnp.max(largest)
        for axis in (C, X, XH, Y, Z):
            scale = lax.pmax(scale, axis)
        scale = scale + 1e-06
        return jnp.sum(pieces.astype(jnp.float32), axis=0) / scale


def solution(mesh):
    torus = Mesh(mesh.devices.reshape(2, 12, 2, 2, 8), (X, Z, C, XH, Y))
    placed = (P(DP, None), P(), P(None, TP), P(TP, DP, None), P(DP, TP), P(DP))
    return jax.shard_map(
        per_device, mesh=torus, in_specs=placed, out_specs=P(DP, TP), check_vma=False
    )
```

time: 324 us -> 187 us (0.58)
  the two profiles are of different devices: /device:TPU:1 before, /device:TPU:2 now
where the time goes in v1:
time: 187 us; the launch traced here: 186 us
  blocking collectives  95.4 us (51%)
  starting transfers between devices  30.7 us (16%)
  waiting for transfers between devices  27.5 us (15%)
  Pallas kernels  22.2 us (12%)
  other arithmetic  6.12 us (3%)
  local copies, waits for them, and re-layouts  3.48 us (2%)
    pmax x5, blocking collectives, per_device(): scale = lax.pmax(scale, axis)  55.9 us
    all_to_all x1, blocking collectives, exchange(): return lax.all_to_all(array, axes, split_axis=0, concat_axis=0, tiled=True)  29.5 us
    ppermute x6, starting transfers between devices, to_peer(): return lax.ppermute(array, XC, [(p, p ^ k) for p in range(4)])  18.1 us
    ppermute x6, waiting for transfers between devices, to_peer(): return lax.ppermute(array, XC, [(p, p ^ k) for p in range(4)])  16.5 us
    all_to_all x2, starting transfers between devices, exchange(): return lax.all_to_all(array, axes, split_axis=0, concat_axis=0, tiled=True)  12.6 us
    all_to_all x2, waiting for transfers between devices, exchange(): return lax.all_to_all(array, axes, split_axis=0, concat_axis=0, tiled=True)  11 us
    all_gather x1, blocking collectives, per_device(): rows = lax.all_gather(arrived, XC, axis=0, tiled=True)  10.1 us
    pallas_call x1, Pallas kernels, split_columns(): pl.pallas_call(split_kernel, out_shape=jax.ShapeDtypeStruct((parts, rows,...  9.52 us
  transfers between devices with their start and end apart: 8, of which 3 were waited for; matrix products, arithmetic and copies ran while one was open for 4% of the time, Pallas kernels for 3%

profile of v1, /device:TPU:2, one launch (start us, length us, event | category | flops | bytes accessed | tf_op | source)
XLA Modules:
  0.0 186.2 jit_solution(5281790983857920717)
XLA Ops:
  0.0 9.5 %split_columns.1 = bf16[16,144,512]{2,1,0:T(8,128)(2,1)} custom-call(bf16[144,8192]{1,0:T(8,128)(2,1)} %bitcast.19), custom_call_target="tpu_custom_call" | custom-call | bytes 4718592 | tf_op jit(solution)/shard_map/terms/split_columns/pallas_call | solution.py:37
  9.5 0.0 copy-start.1
  9.5 8.9 %all-to-all-start = ((bf16[16,144,512]{2,1,0:T(8,128)(2,1)}), bf16[16,144,512]{2,1,0:T(8,128)(2,1)S(1)}, u32[]{:S(2)}, u32[]{:S(2)}) async-start(bf16[16,144,512]{2,1,0:T(8,128)(2,1)} %split_columns.1), calls=%async_computation | async-start | bytes 4718592 | tf_op jit(solution)/shard_map/terms/all_to_all | solution.py:19
  18.4 0.0 copy-done.1
  18.4 0.6 broadcast_in_dim.30.refs_2_
  19.1 0.0 copy-start.2
  19.1 5.0 %student.1 = (bf16[144,512]{1,0:T(8,128)(2,1)}, bf16[4,144,864]{2,1,0:T(8,128)(2,1)}) custom-call(s32[1]{0:T(128)} %bitcast.refs_0_.me_ref, bf16[144,3456]{1,0:T(8,128)(2,1)} %refs_1_.1, f32[1,3456]{1,0:T(1,128)} %broadcast_in_dim.30.refs_2_, bf16[3456,512]{1,0:T(8,128)(2,1)} %refs_3_.1), custom_call_target="tpu_custom_call" | custom-call | flops 509607936 | bytes 3538944 | tf_op jit(solution)/shard_map/student/student/pallas_call | solution.py:68
  24.1 2.5 %collective-permute-start.2 = (bf16[144,512]{1,0:T(8,128)(2,1)}, bf16[144,512]{1,0:T(8,128)(2,1)S(1)}, u32[]{:S(2)}, u32[]{:S(2)}) collective-permute-start(bf16[144,512]{1,0:T(8,128)(2,1)} %get-tuple-element.14), channel_id=1, source_target_pairs={{0,400},{16,384},{384,16},{400,0},{1,401},{17,385},{385,17},{401,1... | collective-permute-start | bytes 442376 | tf_op jit(solution)/shard_map/student/ppermute | solution.py:23
  26.6 5.8 %collective-permute-start.1 = (bf16[144,512]{1,0:T(8,128)(2,1)}, bf16[144,512]{1,0:T(8,128)(2,1)S(1)}, u32[]{:S(2)}, u32[]{:S(2)}) collective-permute-start(bf16[144,512]{1,0:T(8,128)(2,1)} %get-tuple-element.14), channel_id=1, source_target_pairs={{0,384},{16,400},{384,0},{400,16},{1,385},{17,401},{385,1},{401,17... | collective-permute-start | bytes 442376 | tf_op jit(solution)/shard_map/student/ppermute | solution.py:23
  32.4 2.0 %collective-permute-start = (bf16[144,512]{1,0:T(8,128)(2,1)}, bf16[144,512]{1,0:T(8,128)(2,1)S(1)}, u32[]{:S(2)}, u32[]{:S(2)}) collective-permute-start(bf16[144,512]{1,0:T(8,128)(2,1)} %get-tuple-element.14), channel_id=1, source_target_pairs={{0,16},{16,0},{384,400},{400,384},{1,17},{17,1},{385,401},{401,385... | collective-permute-start | bytes 442376 | tf_op jit(solution)/shard_map/student/ppermute | solution.py:23
  34.4 1.4 fusion.2
  35.8 3.3 %collective-permute-start.5 = (bf16[144,864]{1,0:T(8,128)(2,1)S(1)}, bf16[144,864]{1,0:T(8,128)(2,1)S(1)}, u32[]{:S(2)}, u32[]{:S(2)}) collective-permute-start(bf16[144,864]{1,0:T(8,128)(2,1)S(1)} %get-tuple-element.26), channel_id=1, source_target_pairs={{0,400},{16,384},{384,16},{400,0},{1,401},{17,385},{385,17},{401,1... | collective-permute-start | bytes 746504 | tf_op jit(solution)/shard_map/student/ppermute | solution.py:23
  39.1 2.6 %collective-permute-start.4 = (bf16[144,864]{1,0:T(8,128)(2,1)S(1)}, bf16[144,864]{1,0:T(8,128)(2,1)S(1)}, u32[]{:S(2)}, u32[]{:S(2)}) collective-permute-start(bf16[144,864]{1,0:T(8,128)(2,1)S(1)} %get-tuple-element.27), channel_id=1, source_target_pairs={{0,384},{16,400},{384,0},{400,16},{1,385},{17,401},{385,1},{401,17... | collective-permute-start | bytes 746504 | tf_op jit(solution)/shard_map/student/ppermute | solution.py:23
  41.7 0.0 copy-done.2
  41.7 0.7 select_convert_fusion.marks_ref
  42.5 0.2 convert_reduce_fusion.1
  42.7 0.0 collective-permute-done.2
  42.7 1.9 %collective-permute-start.3 = (bf16[144,864]{1,0:T(8,128)(2,1)S(1)}, bf16[144,864]{1,0:T(8,128)(2,1)S(1)}, u32[]{:S(2)}, u32[]{:S(2)}) collective-permute-start(bf16[144,864]{1,0:T(8,128)(2,1)S(1)} %get-tuple-element.28), channel_id=1, source_target_pairs={{0,16},{16,0},{384,400},{400,384},{1,17},{17,1},{385,401},{401,385... | collective-permute-start | bytes 746504 | tf_op jit(solution)/shard_map/student/ppermute | solution.py:23
  44.6 0.0 collective-permute-done.1
  44.6 0.0 collective-permute-done
  44.7 1.8 pad_maximum_fusion.1.pred_ref
  46.5 5.3 %collective-permute-done.5 = bf16[144,864]{1,0:T(8,128)(2,1)S(1)} collective-permute-done((bf16[144,864]{1,0:T(8,128)(2,1)S(1)}, bf16[144,864]{1,0:T(8,128)(2,1)S(1)}, u32[]{:S(2)}, u32[]{:S(2)}) %collective-permute-start.5) | collective-permute-done | bytes 248864 | tf_op jit(solution)/shard_map/student/ppermute | solution.py:23
  51.7 11.3 %collective-permute-done.4 = bf16[144,864]{1,0:T(8,128)(2,1)S(1)} collective-permute-done((bf16[144,864]{1,0:T(8,128)(2,1)S(1)}, bf16[144,864]{1,0:T(8,128)(2,1)S(1)}, u32[]{:S(2)}, u32[]{:S(2)}) %collective-permute-start.4) | collective-permute-done | bytes 248864 | tf_op jit(solution)/shard_map/student/ppermute | solution.py:23
  63.0 0.0 collective-permute-done.3
  63.0 1.2 pad_maximum_fusion.normed_ref
  64.1 11.0 %all-to-all-done.terms_ref = bf16[16,144,512]{2,1,0:T(8,128)(2,1)S(1)} async-done(((bf16[16,144,512]{2,1,0:T(8,128)(2,1)}), bf16[16,144,512]{2,1,0:T(8,128)(2,1)S(1)}, u32[]{:S(2)}, u32[]{:S(2)}) %all-to-all-start) | async-done | bytes 2359328 | tf_op jit(solution)/shard_map/terms/all_to_all | solution.py:19
  75.1 0.0 copy-start
  75.1 0.9 copy.8.slot_ref
  76.0 0.6 copy-done
  76.5 3.0 %teacher_rows.1 = bf16[192,640]{1,0:T(8,128)(2,1)} custom-call(bf16[16,144,512]{2,1,0:T(8,128)(2,1)} %copy-done, bf16[144,512]{1,0:T(8,128)(2,1)} %residual_ref.1, s32[144,1]{1,0:T(8,128)} %copy.8.slot_ref, bf16[144,128]{1,0:T(8,128)(2,1)} %select_convert_fusion.marks_ref), custom_call_target="tpu_custom_call" | custom-call | flops 28311552 | bytes 2359296 | tf_op jit(solution)/shard_map/regroup/teacher_rows/pallas_call | solution.py:100
  79.6 29.5 %all_to_all.15 = bf16[12,16,640]{2,1,0:T(8,128)(2,1)S(1)} all-to-all(bf16[12,16,640]{2,1,0:T(8,128)(2,1)} %bitcast.21), channel_id=1, replica_groups=mesh['dp_0'=2,'dp_1'=12,'dp_2'=2,'tp_0'=2,'tp_1'=8] {'dp_1'}, dimensions={0} | all-to-all | bytes 491520 | tf_op jit(solution)/shard_map/regroup/all_to_all | solution.py:19
  109.1 10.1 %all_gather.3.rows_ref = bf16[768,640]{1,0:T(8,128)(2,1)} all-gather(bf16[192,640]{1,0:T(8,128)(2,1)S(1)} %bitcast.20), channel_id=1, replica_groups=mesh['dp_0'=2,'dp_1'=12,'dp_2'=2,'tp_0'=2,'tp_1'=8] {'dp_0','dp_2'}, dimensions={0}, use_global_device_ids=true | all-gather | bytes 1228800 | tf_op jit(solution)/shard_map/regroup/all_gather | solution.py:189
  119.1 4.6 %gradient.1 = (bf16[864,512]{1,0:T(8,128)(2,1)}, f32[8,128]{1,0:T(8,128)}) custom-call(s32[1]{0:T(128)} %bitcast.refs_0_.me_ref, bf16[768,640]{1,0:T(8,128)(2,1)} %all_gather.3.rows_ref, bf16[4,144,512]{2,1,0:T(8,128)(2,1)} %pad_maximum_fusion.1.pred_ref, bf16[4,144,864]{2,1,0:T(8,128)(2,1)} %pad_maximum_fusion.normed_ref), custom_call_target="tpu_custom_call" | custom-call | flops 1019215872 | bytes 1990656 | tf_op jit(solution)/shard_map/grad/gradient/pallas_call | solution.py:136
  123.7 3.7 %all-to-all-start.2 = ((bf16[12,72,512]{2,1,0:T(8,128)(2,1)}), bf16[12,72,512]{2,1,0:T(8,128)(2,1)S(1)}, u32[]{:S(2)}, u32[]{:S(2)}) async-start(bf16[12,72,512]{2,1,0:T(8,128)(2,1)} %bitcast.22), calls=%async_computation.2 | async-start | bytes 1769472 | tf_op jit(solution)/shard_map/grad/all_to_all | solution.py:19
  127.4 1.4 reduce_max.9
  128.8 3.1 %pmax.35 = f32[]{:T(128)} all-reduce(f32[]{:T(128)} %reduce_max.9), channel_id=1, replica_groups=mesh['dp_0'=2,'dp_1'=12,'dp_2'=2,'tp_0'=2,'tp_1'=8] {'dp_2'}, use_global_device_ids=true, to_apply=%region_3.4 | all-reduce | flops 1 | bytes 8 | tf_op jit(solution)/shard_map/grad/pmax | solution.py:196
  131.9 5.6 %pmax.36 = f32[]{:T(128)} all-reduce(f32[]{:T(128)} %pmax.35), channel_id=1, replica_groups=mesh['dp_0'=2,'dp_1'=12,'dp_2'=2,'tp_0'=2,'tp_1'=8] {'dp_0'}, use_global_device_ids=true, to_apply=%region_4.5 | all-reduce | flops 1 | bytes 8 | tf_op jit(solution)/shard_map/grad/pmax | solution.py:196
  137.5 7.1 %pmax.37 = f32[]{:T(128)} all-reduce(f32[]{:T(128)} %pmax.36), channel_id=1, replica_groups=mesh['dp_0'=2,'dp_1'=12,'dp_2'=2,'tp_0'=2,'tp_1'=8] {'tp_0'}, use_global_device_ids=true, to_apply=%region_5.6 | all-reduce | flops 1 | bytes 8 | tf_op jit(solution)/shard_map/grad/pmax | solution.py:196
  144.5 15.3 %pmax.38 = f32[]{:T(128)} all-reduce(f32[]{:T(128)} %pmax.37), channel_id=1, replica_groups=mesh['dp_0'=2,'dp_1'=12,'dp_2'=2,'tp_0'=2,'tp_1'=8] {'tp_1'}, use_global_device_ids=true, to_apply=%region_6.7 | all-reduce | flops 1 | bytes 8 | tf_op jit(solution)/shard_map/grad/pmax | solution.py:196
  159.8 24.9 %pmax.39 = f32[]{:T(128)} all-reduce(f32[]{:T(128)} %pmax.38), channel_id=1, replica_groups=mesh['dp_0'=2,'dp_1'=12,'dp_2'=2,'tp_0'=2,'tp_1'=8] {'dp_1'}, use_global_device_ids=true, to_apply=%region_7.8 | all-reduce | flops 1 | bytes 8 | tf_op jit(solution)/shard_map/grad/pmax | solution.py:196
  185.3 0.0 all-to-all-done.2
  185.4 0.1 convert_reduce_fusion
  185.5 0.7 broadcast_divide_fusion
  (4 shorter events, 0.1 us)
Async XLA Ops:
  9.5 8.9 %copy-start.1 = (f32[3456]{0:T(1024)S(1)}, f32[3456]{0:T(1024)}, u32[]{:S(2)}) copy-start(f32[3456]{0:T(1024)} %param.7) | copy-start | bytes 41476
  9.5 65.6 %all-to-all-start = ((bf16[16,144,512]{2,1,0:T(8,128)(2,1)}), bf16[16,144,512]{2,1,0:T(8,128)(2,1)S(1)}, u32[]{:S(2)}, u32[]{:S(2)}) async-start(bf16[16,144,512]{2,1,0:T(8,128)(2,1)} %split_columns.1), calls=%async_computation | async-start | bytes 4718592 | tf_op jit(solution)/shard_map/terms/all_to_all | solution.py:19
  19.1 22.6 %copy-start.2 = (s32[144]{0:T(256)S(1)}, s32[144]{0:T(256)}, u32[]{:S(2)}) copy-start(s32[144]{0:T(256)} %param.11) | copy-start | bytes 1732
  24.1 18.6 %collective-permute-start.2 = (bf16[144,512]{1,0:T(8,128)(2,1)}, bf16[144,512]{1,0:T(8,128)(2,1)S(1)}, u32[]{:S(2)}, u32[]{:S(2)}) collective-permute-start(bf16[144,512]{1,0:T(8,128)(2,1)} %get-tuple-element.14), channel_id=1, source_target_pairs={{0,400},{16,384},{384,16},{400,0},{1,401},{17,385},{385,17},{401,1... | collective-permute-start | bytes 442376 | tf_op jit(solution)/shard_map/student/ppermute | solution.py:23
  26.6 18.1 %collective-permute-start.1 = (bf16[144,512]{1,0:T(8,128)(2,1)}, bf16[144,512]{1,0:T(8,128)(2,1)S(1)}, u32[]{:S(2)}, u32[]{:S(2)}) collective-permute-start(bf16[144,512]{1,0:T(8,128)(2,1)} %get-tuple-element.14), channel_id=1, source_target_pairs={{0,384},{16,400},{384,0},{400,16},{1,385},{17,401},{385,1},{401,17... | collective-permute-start | bytes 442376 | tf_op jit(solution)/shard_map/student/ppermute | solution.py:23
  32.4 12.3 %collective-permute-start = (bf16[144,512]{1,0:T(8,128)(2,1)}, bf16[144,512]{1,0:T(8,128)(2,1)S(1)}, u32[]{:S(2)}, u32[]{:S(2)}) collective-permute-start(bf16[144,512]{1,0:T(8,128)(2,1)} %get-tuple-element.14), channel_id=1, source_target_pairs={{0,16},{16,0},{384,400},{400,384},{1,17},{17,1},{385,401},{401,385... | collective-permute-start | bytes 442376 | tf_op jit(solution)/shard_map/student/ppermute | solution.py:23
  35.8 15.9 %collective-permute-start.5 = (bf16[144,864]{1,0:T(8,128)(2,1)S(1)}, bf16[144,864]{1,0:T(8,128)(2,1)S(1)}, u32[]{:S(2)}, u32[]{:S(2)}) collective-permute-start(bf16[144,864]{1,0:T(8,128)(2,1)S(1)} %get-tuple-element.26), channel_id=1, source_target_pairs={{0,400},{16,384},{384,16},{400,0},{1,401},{17,385},{385,17},{401,1... | collective-permute-start | bytes 746504 | tf_op jit(solution)/shard_map/student/ppermute | solution.py:23
  39.1 23.9 %collective-permute-start.4 = (bf16[144,864]{1,0:T(8,128)(2,1)S(1)}, bf16[144,864]{1,0:T(8,128)(2,1)S(1)}, u32[]{:S(2)}, u32[]{:S(2)}) collective-permute-start(bf16[144,864]{1,0:T(8,128)(2,1)S(1)} %get-tuple-element.27), channel_id=1, source_target_pairs={{0,384},{16,400},{384,0},{400,16},{1,385},{17,401},{385,1},{401,17... | collective-permute-start | bytes 746504 | tf_op jit(solution)/shard_map/student/ppermute | solution.py:23
  42.7 20.3 %collective-permute-start.3 = (bf16[144,864]{1,0:T(8,128)(2,1)S(1)}, bf16[144,864]{1,0:T(8,128)(2,1)S(1)}, u32[]{:S(2)}, u32[]{:S(2)}) collective-permute-start(bf16[144,864]{1,0:T(8,128)(2,1)S(1)} %get-tuple-element.28), channel_id=1, source_target_pairs={{0,16},{16,0},{384,400},{400,384},{1,17},{17,1},{385,401},{401,385... | collective-permute-start | bytes 746504 | tf_op jit(solution)/shard_map/student/ppermute | solution.py:23
  75.1 1.4 copy-start
  123.7 61.6 %all-to-all-start.2 = ((bf16[12,72,512]{2,1,0:T(8,128)(2,1)}), bf16[12,72,512]{2,1,0:T(8,128)(2,1)S(1)}, u32[]{:S(2)}, u32[]{:S(2)}) async-start(bf16[12,72,512]{2,1,0:T(8,128)(2,1)} %bitcast.22), calls=%async_computation.2 | async-start | bytes 1769472 | tf_op jit(solution)/shard_map/grad/all_to_all | solution.py:19

commit v2 on v1

v2 whole, which is shorter than its diff:
```python
import jax
import jax.numpy as jnp
from jax import lax
from jax.experimental import pallas as pl
from jax.experimental.pallas import tpu as pltpu
from jax.sharding import Mesh
from jax.sharding import PartitionSpec as P

X, ZH, ZL, C = "x_lo", "z_hi", "z_lo", "core"
XH, Y = "x_hi", "y"
DP, TP, XC, Z = (X, ZH, ZL, C), (XH, Y), (X, C), (ZH, ZL)
VMEM = pl.BlockSpec(memory_space=pltpu.VMEM)
SMEM = pl.BlockSpec(memory_space=pltpu.SMEM)
ROWS_FIRST = (((0,), (0,)), ((), ()))
MARKS, FULL, REST = 128, 8, 4


def exchange(array, axes):
    return lax.all_to_all(array, axes, split_axis=0, concat_axis=0, tiled=True)


def to_peer(array, k):
    return lax.ppermute(array, XC, [(p, p ^ k) for p in range(4)])


def cost(flops, moved):
    return pl.CostEstimate(flops=flops, bytes_accessed=moved, transcendentals=0)


def split_kernel(in_ref, out_ref):
    parts, _, columns = out_ref.shape
    for k in range(parts):
        out_ref[k] = in_ref[:, k * columns : (k + 1) * columns]


def split_columns(array, parts):
    rows, width = array.shape
    return pl.pallas_call(
        split_kernel,
        out_shape=jax.ShapeDtypeStruct((parts, rows, width // parts), array.dtype),
        in_specs=[VMEM],
        out_specs=VMEM,
        name="split_columns",
        cost_estimate=cost(0, 4 * rows * width),
    )(array)


def student_kernel(sizes, me_ref, hidden_ref, gain_ref, proj_ref, pred_ref, parts_ref, wide_ref, part_ref):
    nx, nz, nc, block = sizes
    values = hidden_ref[...].astype(jnp.float32)
    inverse = lax.rsqrt(jnp.mean(values * values, axis=-1, keepdims=True) + 1e-05)
    normed = values * inverse * gain_ref[...]
    pred = jnp.dot(normed.astype(jnp.bfloat16), proj_ref[...], preferred_element_type=jnp.float32)
    pred_ref[...] = pred.astype(jnp.bfloat16)
    wide_ref[...] = normed
    for p in range(nx * nc):
        x, c = p // nc, p % nc
        for z in range(nz):
            start = ((x * nz + z) * nc + c) * block
            part_ref[:, z * block : (z + 1) * block] = wide_ref[:, start : start + block]
        parts_ref[p ^ me_ref[0]] = part_ref[...].astype(jnp.bfloat16)


def student(me, hidden, gain, projection, sizes):
    nx, nz, nc, block = sizes
    rows, features = hidden.shape
    columns = projection.shape[1]
    return pl.pallas_call(
        lambda *refs: student_kernel(sizes, *refs),
        out_shape=(
            jax.ShapeDtypeStruct((rows, columns), jnp.bfloat16),
            jax.ShapeDtypeStruct((nx * nc, rows, nz * block), jnp.bfloat16),
        ),
        in_specs=[SMEM, VMEM, VMEM, VMEM],
        out_specs=(VMEM, VMEM),
        scratch_shapes=[
            pltpu.VMEM((rows, features), jnp.float32),
            pltpu.VMEM((rows, nz * block), jnp.float32),
        ],
        name="student",
        cost_estimate=cost(2 * rows * features * columns, 2 * features * columns),
    )(me, hidden, gain, projection)


def teacher_kernel(terms_ref, residual_ref, slots_ref, marks_ref, out_ref):
    count, rows, columns = terms_ref.shape
    half = columns // 2
    summed = terms_ref[0].astype(jnp.float32)
    for k in range(1, count):
        summed = summed + terms_ref[k].astype(jnp.float32)
    teacher = (residual_ref[...].astype(jnp.float32) + summed).astype(jnp.bfloat16)
    lines = lax.broadcasted_iota(jnp.int32, (out_ref.shape[0], rows), 0)
    full, low, high = (
        (lines == slots_ref[k : k + 1, :]).astype(jnp.float32).astype(jnp.bfloat16) for k in range(3)
    )

    def moved(select, part):
        return jnp.dot(select, part, preferred_element_type=jnp.float32)

    rest = moved(low, teacher[:, :half]) + moved(high, teacher[:, half:])
    out_ref[:, :columns] = moved(full, teacher).astype(jnp.bfloat16)
    out_ref[:, columns : columns + half] = rest.astype(jnp.bfloat16)
    out_ref[:, columns + half :] = moved(full + low + high, marks_ref[...]).astype(jnp.bfloat16)


def teacher_rows(terms, residual, slots, marks, lines):
    rows, columns = residual.shape
    width = columns + columns // 2 + MARKS
    return pl.pallas_call(
        teacher_kernel,
        out_shape=jax.ShapeDtypeStruct((lines, width), jnp.bfloat16),
        in_specs=[VMEM] * 4,
        out_specs=VMEM,
        name="teacher_rows",
        cost_estimate=cost(2 * rows * width * lines, 2 * terms.size),
    )(terms, residual, slots, marks)


def gradient_kernel(me_ref, rows_ref, pred_ref, normed_ref, sum_ref, max_ref):
    groups, per, height = normed_ref.shape
    columns = pred_ref.shape[-1]
    half = columns // 2
    lines, tokens = rows_ref.shape[0], groups * per
    marks = rows_ref[:, columns + half :].astype(jnp.float32).astype(jnp.int32)
    lanes = lax.broadcasted_iota(jnp.int32, (lines, tokens), 1)
    line = lax.broadcasted_iota(jnp.int32, (lines, tokens), 0)
    low_half = (line & (FULL - 1)) < REST

    def select(at, wanted):
        place = (marks[:, at : at + 1] ^ me_ref[0]) * per + marks[:, at + 1 : at + 2]
        return ((lanes == place) & wanted).astype(jnp.float32).astype(jnp.bfloat16)

    def placed(chosen, start):
        return lax.dot_general(
            chosen, rows_ref[:, start : start + half], ROWS_FIRST, preferred_element_type=jnp.float32
        )

    full = select(0, True)
    target = [
        placed(full, 0) + placed(select(2, low_half), columns),
        placed(full, half) + placed(select(2, ~low_half), columns),
    ]
    largest = jnp.zeros((1, 1), jnp.float32)
    for side in range(2):
        cols = slice(side * half, (side + 1) * half)
        total = None
        for g in range(groups):
            aimed = target[side][g * per : (g + 1) * per]
            diff = (pred_ref[g, :, cols].astype(jnp.float32) - aimed).astype(jnp.bfloat16)
            part = lax.dot_general(normed_ref[g], diff, ROWS_FIRST, preferred_element_type=jnp.float32)
            largest = jnp.maximum(largest, jnp.max(jnp.abs(part), keepdims=True))
            total = part if total is None else total + part
        sum_ref[:, cols] = total.astype(jnp.bfloat16)
    max_ref[0, 0] = jnp.max(largest)


def gradient(me, rows, pred, normed):
    groups, per, height = normed.shape
    columns = pred.shape[-1]
    return pl.pallas_call(
        gradient_kernel,
        out_shape=(
            jax.ShapeDtypeStruct((height, columns), jnp.bfloat16),
            jax.ShapeDtypeStruct((1, 1), jnp.float32),
        ),
        in_specs=[SMEM, VMEM, VMEM, VMEM],
        out_specs=(VMEM, SMEM),
        name="gradient",
        cost_estimate=cost(4 * groups * per * height * columns, 4 * normed.size),
    )(me, rows, pred, normed)


def per_device(student_hidden, norm_gain, projection, teacher_partials, teacher_residual, owner):
    rows_dev, columns = teacher_residual.shape
    features = student_hidden.shape[1]
    nx, nz, nc = (lax.axis_size(a) for a in (X, Z, C))
    peers = nx * nc
    block = features // (nx * nz * nc)
    assert rows_dev == nz * (FULL + REST)
    me = lax.axis_index(X) * nc + lax.axis_index(C)
    me_ref = me.reshape(1).astype(jnp.int32)

    with jax.named_scope("terms"):
        terms = exchange(split_columns(teacher_partials[0], lax.axis_size(TP)), TP)

    with jax.named_scope("student"):
        sizes = (nx, nz, nc, block)
        pred, parts = student(me_ref, student_hidden, norm_gain[None], projection, sizes)
        pred_parts = [pred] + [to_peer(pred, k) for k in range(1, peers)]
        normed_parts = [parts[0]] + [to_peer(parts[k], k) for k in range(1, peers)]
        pred_all, normed_all = jnp.stack(pred_parts), jnp.stack(normed_parts)

    with jax.named_scope("places"):
        whose = owner // rows_dev
        z_to = (whose // nc) % nz
        peer_to = (whose // (nz * nc)) * nc + whose % nc
        index = jnp.arange(rows_dev)
        earlier = (z_to[None, :] == z_to[:, None]) & (index[None, :] < index[:, None])
        rank = jnp.sum(earlier.astype(jnp.int32), axis=1)
        full = rank < FULL
        line = z_to * FULL + jnp.where(full, rank, rank - FULL)
        slots = jnp.stack([jnp.where(full, line, -1), jnp.where(full, -1, line)])
        slots = jnp.concatenate([slots, jnp.where(full, -1, line + REST)[None]])
        lane = lax.broadcasted_iota(jnp.int32, (rows_dev, MARKS), 1) - jnp.where(full, 0, 2)[:, None]
        marks = jnp.where(lane == 0, peer_to[:, None], (owner % rows_dev)[:, None])
        marks = jnp.where((lane == 0) | (lane == 1), marks, 0).astype(jnp.bfloat16)

    terms, pred_all, normed_all = lax.optimization_barrier((terms, pred_all, normed_all))

    with jax.named_scope("regroup"):
        outgoing = teacher_rows(terms, teacher_residual, slots, marks, nz * FULL)
        arrived = exchange(outgoing.reshape(nz, FULL, -1), Z).reshape(nz * FULL, -1)
        rows = lax.all_gather(arrived, XC, axis=0, tiled=True)

    with jax.named_scope("grad"):
        tile, largest = gradient(me_ref, rows, pred_all, normed_all)
        pieces = exchange(tile.reshape(nz, block, columns), Z)
        scale = largest[0, 0]
        for axes in (C, (XH, X), Y, ZL, ZH):
            scale = lax.pmax(scale, axes)
        scale = scale + 1e-06
        return jnp.sum(pieces.astype(jnp.float32), axis=0) / scale


def solution(mesh):
    torus = Mesh(mesh.devices.reshape(2, 3, 4, 2, 2, 8), (X, ZH, ZL, C, XH, Y))
    placed = (P(DP, None), P(), P(None, TP), P(TP, DP, None), P(DP, TP), P(DP))
    return jax.shard_map(
        per_device, mesh=torus, in_specs=placed, out_specs=P(DP, TP), check_vma=False
    )
```

time: 187 us -> 173 us (0.925)
  the two profiles are of different devices: /device:TPU:2 before, /device:TPU:24 now
where the time goes in v2:
time: 173 us; the launch traced here: 172 us
  blocking collectives  90.7 us (52%)
  starting transfers between devices  31.7 us (18%)
  waiting for transfers between devices  23.8 us (14%)
  Pallas kernels  15.9 us (9%)
  other arithmetic  5.36 us (3%)
  local copies, waits for them, and re-layouts  3.45 us (2%)
    pmax x5, blocking collectives, per_device(): scale = lax.pmax(scale, axes)  55.4 us
    all_to_all x1, blocking collectives, exchange(): return lax.all_to_all(array, axes, split_axis=0, concat_axis=0, tiled=True)  27.7 us
    ppermute x6, waiting for transfers between devices, to_peer(): return lax.ppermute(array, XC, [(p, p ^ k) for p in range(4)])  17.3 us
    all_to_all x2, starting transfers between devices, exchange(): return lax.all_to_all(array, axes, split_axis=0, concat_axis=0, tiled=True)  16.6 us
    ppermute x6, starting transfers between devices, to_peer(): return lax.ppermute(array, XC, [(p, p ^ k) for p in range(4)])  15.2 us
    all_gather x1, blocking collectives, per_device(): rows = lax.all_gather(arrived, XC, axis=0, tiled=True)  7.6 us
    all_to_all x2, waiting for transfers between devices, exchange(): return lax.all_to_all(array, axes, split_axis=0, concat_axis=0, tiled=True)  6.49 us
    pallas_call x1, Pallas kernels, student(): pl.pallas_call(lambda *refs: student_kernel(sizes, *refs), out_shape=(jax...  5.02 us
  transfers between devices with their start and end apart: 8, of which 2 were waited for; matrix products, arithmetic and copies ran while one was open for 4% of the time, Pallas kernels for 3%

profile of v2, /device:TPU:24, one launch (start us, length us, event | category | flops | bytes accessed | tf_op | source)
XLA Modules:
  0.0 171.7 jit_solution(13151904389934910743)
XLA Ops:
  0.0 3.2 %split_columns.1 = bf16[16,144,512]{2,1,0:T(8,128)(2,1)} custom-call(bf16[144,8192]{1,0:T(8,128)(2,1)} %bitcast.22), custom_call_target="tpu_custom_call" | custom-call | bytes 4718592 | tf_op jit(solution)/shard_map/terms/split_columns/pallas_call | solution.py:38
  3.2 0.0 copy-start.1
  3.2 12.9 %all-to-all-start = ((bf16[16,144,512]{2,1,0:T(8,128)(2,1)}), bf16[16,144,512]{2,1,0:T(8,128)(2,1)S(1)}, u32[]{:S(2)}, u32[]{:S(2)}) async-start(bf16[16,144,512]{2,1,0:T(8,128)(2,1)} %split_columns.1), calls=%async_computation | async-start | bytes 4718592 | tf_op jit(solution)/shard_map/terms/all_to_all | solution.py:19
  16.1 0.0 copy-done.1
  16.1 0.6 broadcast_in_dim.40.refs_2_
  16.7 0.0 copy-start.2
  16.7 5.0 %student.1 = (bf16[144,512]{1,0:T(8,128)(2,1)}, bf16[4,144,864]{2,1,0:T(8,128)(2,1)}) custom-call(s32[1]{0:T(128)} %bitcast.refs_0_.me_ref, bf16[144,3456]{1,0:T(8,128)(2,1)} %refs_1_.1, f32[1,3456]{1,0:T(1,128)} %broadcast_in_dim.40.refs_2_, bf16[3456,512]{1,0:T(8,128)(2,1)} %refs_3_.1), custom_call_target="tpu_custom_call" | custom-call | flops 509607936 | bytes 3538944 | tf_op jit(solution)/shard_map/student/student/pallas_call | solution.py:68
  21.7 1.9 %collective-permute-start.2 = (bf16[144,512]{1,0:T(8,128)(2,1)}, bf16[144,512]{1,0:T(8,128)(2,1)S(1)}, u32[]{:S(2)}, u32[]{:S(2)}) collective-permute-start(bf16[144,512]{1,0:T(8,128)(2,1)} %get-tuple-element.12), channel_id=1, source_target_pairs={{0,400},{16,384},{384,16},{400,0},{1,401},{17,385},{385,17},{401,1... | collective-permute-start | bytes 442376 | tf_op jit(solution)/shard_map/student/ppermute | solution.py:23
  23.7 1.9 %collective-permute-start.1 = (bf16[144,512]{1,0:T(8,128)(2,1)}, bf16[144,512]{1,0:T(8,128)(2,1)S(1)}, u32[]{:S(2)}, u32[]{:S(2)}) collective-permute-start(bf16[144,512]{1,0:T(8,128)(2,1)} %get-tuple-element.12), channel_id=1, source_target_pairs={{0,384},{16,400},{384,0},{400,16},{1,385},{17,401},{385,1},{401,17... | collective-permute-start | bytes 442376 | tf_op jit(solution)/shard_map/student/ppermute | solution.py:23
  25.6 3.7 %collective-permute-start = (bf16[144,512]{1,0:T(8,128)(2,1)}, bf16[144,512]{1,0:T(8,128)(2,1)S(1)}, u32[]{:S(2)}, u32[]{:S(2)}) collective-permute-start(bf16[144,512]{1,0:T(8,128)(2,1)} %get-tuple-element.12), channel_id=1, source_target_pairs={{0,16},{16,0},{384,400},{400,384},{1,17},{17,1},{385,401},{401,385... | collective-permute-start | bytes 442376 | tf_op jit(solution)/shard_map/student/ppermute | solution.py:23
  29.3 1.4 fusion.6
  30.8 2.2 %collective-permute-start.5 = (bf16[144,864]{1,0:T(8,128)(2,1)S(1)}, bf16[144,864]{1,0:T(8,128)(2,1)S(1)}, u32[]{:S(2)}, u32[]{:S(2)}) collective-permute-start(bf16[144,864]{1,0:T(8,128)(2,1)S(1)} %get-tuple-element.22), channel_id=1, source_target_pairs={{0,400},{16,384},{384,16},{400,0},{1,401},{17,385},{385,17},{401,1... | collective-permute-start | bytes 746504 | tf_op jit(solution)/shard_map/student/ppermute | solution.py:23
  33.0 3.3 %collective-permute-start.4 = (bf16[144,864]{1,0:T(8,128)(2,1)S(1)}, bf16[144,864]{1,0:T(8,128)(2,1)S(1)}, u32[]{:S(2)}, u32[]{:S(2)}) collective-permute-start(bf16[144,864]{1,0:T(8,128)(2,1)S(1)} %get-tuple-element.23), channel_id=1, source_target_pairs={{0,384},{16,400},{384,0},{400,16},{1,385},{17,401},{385,1},{401,17... | collective-permute-start | bytes 746504 | tf_op jit(solution)/shard_map/student/ppermute | solution.py:23
  36.2 0.0 copy-done.2
  36.3 0.2 convert_reduce_fusion.1
  36.5 0.0 collective-permute-done.2
  36.5 2.1 %collective-permute-start.3 = (bf16[144,864]{1,0:T(8,128)(2,1)S(1)}, bf16[144,864]{1,0:T(8,128)(2,1)S(1)}, u32[]{:S(2)}, u32[]{:S(2)}) collective-permute-start(bf16[144,864]{1,0:T(8,128)(2,1)S(1)} %get-tuple-element.24), channel_id=1, source_target_pairs={{0,16},{16,0},{384,400},{400,384},{1,17},{17,1},{385,401},{401,385... | collective-permute-start | bytes 746504 | tf_op jit(solution)/shard_map/student/ppermute | solution.py:23
  38.7 0.7 select_convert_fusion.marks_ref
  39.4 0.6 pad_add_fusion.slots_ref
  40.0 0.0 collective-permute-done.1
  40.0 0.0 collective-permute-done
  40.0 1.8 %pad_maximum_fusion.1.pred_ref = bf16[4,144,512]{2,1,0:T(8,128)(2,1)} fusion(bf16[1,144,512]{2,1,0:T(8,128)(2,1)S(1)} %bitcast.30, bf16[1,144,512]{2,1,0:T(8,128)(2,1)S(1)} %bitcast.31, bf16[1,144,512]{2,1,0:T(8,128)(2,1)S(1)} %bitcast.32, bf16[1,144,512]{2,1,0:T(8,128)(2,1)} %bitcast.29), kind=kLoop, calls=%fused_computation.2 | loop fusion | flops 884736 | bytes 1179648 | tf_op jit(solution)/shard_map/student/stack | solution.py:191
  41.8 0.0 collective-permute-done.5
  41.8 17.3 %collective-permute-done.4 = bf16[144,864]{1,0:T(8,128)(2,1)S(1)} collective-permute-done((bf16[144,864]{1,0:T(8,128)(2,1)S(1)}, bf16[144,864]{1,0:T(8,128)(2,1)S(1)}, u32[]{:S(2)}, u32[]{:S(2)}) %collective-permute-start.4) | collective-permute-done | bytes 248864 | tf_op jit(solution)/shard_map/student/ppermute | solution.py:23
  59.1 0.0 collective-permute-done.3
  59.1 1.2 pad_maximum_fusion.normed_ref
  60.2 6.5 %all-to-all-done.terms_ref = bf16[16,144,512]{2,1,0:T(8,128)(2,1)S(1)} async-done(((bf16[16,144,512]{2,1,0:T(8,128)(2,1)}), bf16[16,144,512]{2,1,0:T(8,128)(2,1)S(1)}, u32[]{:S(2)}, u32[]{:S(2)}) %all-to-all-start) | async-done | bytes 2359328 | tf_op jit(solution)/shard_map/terms/all_to_all | solution.py:19
  66.7 0.0 copy-start
  66.7 1.4 copy-done
  68.1 3.0 %teacher_rows.1 = bf16[96,896]{1,0:T(8,128)(2,1)} custom-call(bf16[16,144,512]{2,1,0:T(8,128)(2,1)} %copy-done, bf16[144,512]{1,0:T(8,128)(2,1)} %residual_ref.1, s32[3,144]{1,0:T(4,128)} %pad_add_fusion.slots_ref, bf16[144,128]{1,0:T(8,128)(2,1)} %select_convert_fusion.marks_ref), custom_call_target="tpu_custom_call" | custom-call | flops 24772608 | bytes 2359296 | tf_op jit(solution)/shard_map/regroup/teacher_rows/pallas_call | solution.py:109
  71.1 27.7 %all_to_all.15 = bf16[12,8,896]{2,1,0:T(8,128)(2,1)S(1)} all-to-all(bf16[12,8,896]{2,1,0:T(8,128)(2,1)} %bitcast.25), channel_id=1, replica_groups=mesh['x_lo'=2,'z_hi'=3,'z_lo'=4,'core'=2,'x_hi'=2,'y'=8] {'z_hi','z_lo'}, dimensions={0} | all-to-all | bytes 344064 | tf_op jit(solution)/shard_map/regroup/all_to_all | solution.py:19
  98.8 7.6 %all_gather.3.rows_ref = bf16[384,896]{1,0:T(8,128)(2,1)} all-gather(bf16[96,896]{1,0:T(8,128)(2,1)S(1)} %bitcast.24), channel_id=1, replica_groups=mesh['x_lo'=2,'z_hi'=3,'z_lo'=4,'core'=2,'x_hi'=2,'y'=8] {'x_lo','core'}, dimensions={0}, use_global_device_ids=true | all-gather | bytes 860160 | tf_op jit(solution)/shard_map/regroup/all_gather | solution.py:213
  106.4 4.7 %gradient.1 = (bf16[864,512]{1,0:T(8,128)(2,1)}, f32[1,1]{1,0:T(1,128)}) custom-call(s32[1]{0:T(128)} %bitcast.refs_0_.me_ref, bf16[384,896]{1,0:T(8,128)(2,1)} %all_gather.3.rows_ref, bf16[4,144,512]{2,1,0:T(8,128)(2,1)} %pad_maximum_fusion.1.pred_ref, bf16[4,144,864]{2,1,0:T(8,128)(2,1)} %pad_maximum_fusion.normed_ref), custom_call_target="tpu_custom_call" | custom-call | flops 1019215872 | bytes 1990656 | tf_op jit(solution)/shard_map/grad/gradient/pallas_call | solution.py:160
  111.1 3.7 %all-to-all-start.2 = ((bf16[12,72,512]{2,1,0:T(8,128)(2,1)}), bf16[12,72,512]{2,1,0:T(8,128)(2,1)S(1)}, u32[]{:S(2)}, u32[]{:S(2)}) async-start(bf16[12,72,512]{2,1,0:T(8,128)(2,1)} %bitcast.23), calls=%async_computation.2 | async-start | bytes 1769472 | tf_op jit(solution)/shard_map/grad/all_to_all | solution.py:19
  114.8 3.1 %pmax.35 = f32[]{:T(128)} all-reduce(f32[]{:T(128)} %bitcast.18), channel_id=1, replica_groups=mesh['x_lo'=2,'z_hi'=3,'z_lo'=4,'core'=2,'x_hi'=2,'y'=8] {'core'}, use_global_device_ids=true, to_apply=%region_2.3 | all-reduce | flops 1 | bytes 8 | tf_op jit(solution)/shard_map/grad/pmax | solution.py:220
  118.0 11.3 %pmax.36 = f32[]{:T(128)} all-reduce(f32[]{:T(128)} %pmax.35), channel_id=1, replica_groups=mesh['x_lo'=2,'z_hi'=3,'z_lo'=4,'core'=2,'x_hi'=2,'y'=8] {'x_hi','x_lo'}, use_global_device_ids=true, to_apply=%region_3.4 | all-reduce | flops 1 | bytes 8 | tf_op jit(solution)/shard_map/grad/pmax | solution.py:220
  129.3 16.8 %pmax.37 = f32[]{:T(128)} all-reduce(f32[]{:T(128)} %pmax.36), channel_id=1, replica_groups=mesh['x_lo'=2,'z_hi'=3,'z_lo'=4,'core'=2,'x_hi'=2,'y'=8] {'y'}, use_global_device_ids=true, to_apply=%region_4.5 | all-reduce | flops 1 | bytes 8 | tf_op jit(solution)/shard_map/grad/pmax | solution.py:220
  146.1 12.6 %pmax.38 = f32[]{:T(128)} all-reduce(f32[]{:T(128)} %pmax.37), channel_id=1, replica_groups=mesh['x_lo'=2,'z_hi'=3,'z_lo'=4,'core'=2,'x_hi'=2,'y'=8] {'z_lo'}, use_global_device_ids=true, to_apply=%region_5.6 | all-reduce | flops 1 | bytes 8 | tf_op jit(solution)/shard_map/grad/pmax | solution.py:220
  158.7 11.6 %pmax.39 = f32[]{:T(128)} all-reduce(f32[]{:T(128)} %pmax.38), channel_id=1, replica_groups=mesh['x_lo'=2,'z_hi'=3,'z_lo'=4,'core'=2,'x_hi'=2,'y'=8] {'z_hi'}, use_global_device_ids=true, to_apply=%region_6.7 | all-reduce | flops 1 | bytes 8 | tf_op jit(solution)/shard_map/grad/pmax | solution.py:220
  170.9 0.0 all-to-all-done.2
  170.9 0.1 convert_reduce_fusion
  171.0 0.7 broadcast_divide_fusion
  (3 shorter events, 0.1 us)
Async XLA Ops:
  3.2 12.9 %copy-start.1 = (f32[3456]{0:T(1024)S(1)}, f32[3456]{0:T(1024)}, u32[]{:S(2)}) copy-start(f32[3456]{0:T(1024)} %param.7) | copy-start | bytes 41476
  3.2 63.5 %all-to-all-start = ((bf16[16,144,512]{2,1,0:T(8,128)(2,1)}), bf16[16,144,512]{2,1,0:T(8,128)(2,1)S(1)}, u32[]{:S(2)}, u32[]{:S(2)}) async-start(bf16[16,144,512]{2,1,0:T(8,128)(2,1)} %split_columns.1), calls=%async_computation | async-start | bytes 4718592 | tf_op jit(solution)/shard_map/terms/all_to_all | solution.py:19
  16.7 19.5 %copy-start.2 = (s32[144]{0:T(256)S(1)}, s32[144]{0:T(256)}, u32[]{:S(2)}) copy-start(s32[144]{0:T(256)} %param.11) | copy-start | bytes 1732
  21.7 14.8 %collective-permute-start.2 = (bf16[144,512]{1,0:T(8,128)(2,1)}, bf16[144,512]{1,0:T(8,128)(2,1)S(1)}, u32[]{:S(2)}, u32[]{:S(2)}) collective-permute-start(bf16[144,512]{1,0:T(8,128)(2,1)} %get-tuple-element.12), channel_id=1, source_target_pairs={{0,400},{16,384},{384,16},{400,0},{1,401},{17,385},{385,17},{401,1... | collective-permute-start | bytes 442376 | tf_op jit(solution)/shard_map/student/ppermute | solution.py:23
  23.7 16.3 %collective-permute-start.1 = (bf16[144,512]{1,0:T(8,128)(2,1)}, bf16[144,512]{1,0:T(8,128)(2,1)S(1)}, u32[]{:S(2)}, u32[]{:S(2)}) collective-permute-start(bf16[144,512]{1,0:T(8,128)(2,1)} %get-tuple-element.12), channel_id=1, source_target_pairs={{0,384},{16,400},{384,0},{400,16},{1,385},{17,401},{385,1},{401,17... | collective-permute-start | bytes 442376 | tf_op jit(solution)/shard_map/student/ppermute | solution.py:23
  25.6 14.4 %collective-permute-start = (bf16[144,512]{1,0:T(8,128)(2,1)}, bf16[144,512]{1,0:T(8,128)(2,1)S(1)}, u32[]{:S(2)}, u32[]{:S(2)}) collective-permute-start(bf16[144,512]{1,0:T(8,128)(2,1)} %get-tuple-element.12), channel_id=1, source_target_pairs={{0,16},{16,0},{384,400},{400,384},{1,17},{17,1},{385,401},{401,385... | collective-permute-start | bytes 442376 | tf_op jit(solution)/shard_map/student/ppermute | solution.py:23
  30.8 11.1 %collective-permute-start.5 = (bf16[144,864]{1,0:T(8,128)(2,1)S(1)}, bf16[144,864]{1,0:T(8,128)(2,1)S(1)}, u32[]{:S(2)}, u32[]{:S(2)}) collective-permute-start(bf16[144,864]{1,0:T(8,128)(2,1)S(1)} %get-tuple-element.22), channel_id=1, source_target_pairs={{0,400},{16,384},{384,16},{400,0},{1,401},{17,385},{385,17},{401,1... | collective-permute-start | bytes 746504 | tf_op jit(solution)/shard_map/student/ppermute | solution.py:23
  33.0 26.1 %collective-permute-start.4 = (bf16[144,864]{1,0:T(8,128)(2,1)S(1)}, bf16[144,864]{1,0:T(8,128)(2,1)S(1)}, u32[]{:S(2)}, u32[]{:S(2)}) collective-permute-start(bf16[144,864]{1,0:T(8,128)(2,1)S(1)} %get-tuple-element.23), channel_id=1, source_target_pairs={{0,384},{16,400},{384,0},{400,16},{1,385},{17,401},{385,1},{401,17... | collective-permute-start | bytes 746504 | tf_op jit(solution)/shard_map/student/ppermute | solution.py:23
  36.5 22.6 %collective-permute-start.3 = (bf16[144,864]{1,0:T(8,128)(2,1)S(1)}, bf16[144,864]{1,0:T(8,128)(2,1)S(1)}, u32[]{:S(2)}, u32[]{:S(2)}) collective-permute-start(bf16[144,864]{1,0:T(8,128)(2,1)S(1)} %get-tuple-element.24), channel_id=1, source_target_pairs={{0,16},{16,0},{384,400},{400,384},{1,17},{17,1},{385,401},{401,385... | collective-permute-start | bytes 746504 | tf_op jit(solution)/shard_map/student/ppermute | solution.py:23
  66.7 1.4 copy-start
  111.1 59.8 %all-to-all-start.2 = ((bf16[12,72,512]{2,1,0:T(8,128)(2,1)}), bf16[12,72,512]{2,1,0:T(8,128)(2,1)S(1)}, u32[]{:S(2)}, u32[]{:S(2)}) async-start(bf16[12,72,512]{2,1,0:T(8,128)(2,1)} %bitcast.23), calls=%async_computation.2 | async-start | bytes 1769472 | tf_op jit(solution)/shard_map/grad/all_to_all | solution.py:19

commit v3 on v2

v3 whole, which is shorter than its diff:
```python
import jax
import jax.numpy as jnp
from jax import lax
from jax.experimental import pallas as pl
from jax.experimental.pallas import tpu as pltpu
from jax.sharding import Mesh
from jax.sharding import PartitionSpec as P


X, ZH, ZL, C = "x_lo", "z_hi", "z_lo", "core"
XH, Y = "x_hi", "y"
DP, TP, XC, Z = (X, ZH, ZL, C), (XH, Y), (X, C), (ZH, ZL)
VMEM = pl.BlockSpec(memory_space=pltpu.VMEM)
SMEM = pl.BlockSpec(memory_space=pltpu.SMEM)
ROWS_FIRST = (((0,), (0,)), ((), ()))
MARKS, FULL, REST = 128, 8, 4


def exchange(array, axes):
    return lax.all_to_all(array, axes, split_axis=0, concat_axis=0, tiled=True)


def to_peer(array, k):
    return lax.ppermute(array, XC, [(p, p ^ k) for p in range(4)])


def cost(flops, moved):
    return pl.CostEstimate(flops=flops, bytes_accessed=moved, transcendentals=0)


def half_of(array):
    return pl.BlockSpec((array.shape[0], array.shape[1] // 2), lambda _, which: (0, which[0]))


def pieces_of(columns):
    return ((0, columns // 4), (columns // 4, columns))


def split_kernel(_, in_ref, *out_refs):
    columns = sum(ref.shape[-1] for ref in out_refs)
    for ref, (start, stop) in zip(out_refs, pieces_of(columns)):
        for k in range(ref.shape[0]):
            ref[k] = in_ref[:, k * columns + start : k * columns + stop]


def split_columns(which, array, parts, columns):
    rows = array.shape[0]
    shapes = [(parts, rows, stop - start) for start, stop in pieces_of(columns)]
    return pl.pallas_call(
        split_kernel,
        out_shape=[jax.ShapeDtypeStruct(shape, array.dtype) for shape in shapes],
        grid_spec=pltpu.PrefetchScalarGridSpec(
            num_scalar_prefetch=1,
            grid=(1,),
            in_specs=[half_of(array)],
            out_specs=[pl.BlockSpec(shape, lambda *_: (0, 0, 0)) for shape in shapes],
        ),
        name="split_columns",
        cost_estimate=cost(0, 2 * array.size),
    )(which, array)


def pair_kernel(start, columns, _, in_ref, got_ref, out_ref):
    width = got_ref.shape[-1]
    for k in range(got_ref.shape[0]):
        at = k * columns + start
        mine = in_ref[:, at : at + width].astype(jnp.float32)
        out_ref[k] = (mine + got_ref[k].astype(jnp.float32)).astype(jnp.bfloat16)


def pair_sum(which, array, got, start, columns):
    return pl.pallas_call(
        lambda *refs: pair_kernel(start, columns, *refs),
        out_shape=jax.ShapeDtypeStruct(got.shape, got.dtype),
        grid_spec=pltpu.PrefetchScalarGridSpec(
            num_scalar_prefetch=1,
            grid=(1,),
            in_specs=[half_of(array), pl.BlockSpec(got.shape, lambda *_: (0, 0, 0))],
            out_specs=pl.BlockSpec(got.shape, lambda *_: (0, 0, 0)),
        ),
        name="pair_sum",
        cost_estimate=cost(got.size, 6 * got.size),
    )(which, array, got)


def lane_tiles(width):
    return -(-width // 128) * 128


def student_kernel(sizes, me_ref, hidden_ref, gain_ref, proj_ref, *refs):
    nx, nz, nc, block = sizes
    peers = nx * nc
    out_refs, (wide_ref, line_ref, parts_ref) = refs[:peers], refs[peers:]
    values = hidden_ref[...].astype(jnp.float32)
    inverse = lax.rsqrt(jnp.mean(values * values, axis=-1, keepdims=True) + 1e-05)
    normed = values * inverse * gain_ref[...]
    pred = jnp.dot(normed.astype(jnp.bfloat16), proj_ref[...], preferred_element_type=jnp.float32)
    pred = pred.astype(jnp.bfloat16)
    wide_ref[...] = normed
    line_ref[...] = jnp.zeros_like(line_ref)
    for p in range(peers):
        x, c = p // nc, p % nc
        for z in range(nz):
            start = ((x * nz + z) * nc + c) * block
            line_ref[:, z * block : (z + 1) * block] = wide_ref[:, start : start + block]
        parts_ref[p] = line_ref[...].astype(jnp.bfloat16)
    at = line_ref.shape[-1]
    for k in range(peers):
        out_refs[k][:, :at] = parts_ref[me_ref[0] ^ k]
        out_refs[k][:, at:] = pred


def student(me, hidden, gain, projection, sizes):
    nx, nz, nc, block = sizes
    rows, features = hidden.shape
    columns = projection.shape[1]
    peers, wide = nx * nc, lane_tiles(nz * block)
    return pl.pallas_call(
        lambda *refs: student_kernel(sizes, *refs),
        out_shape=[jax.ShapeDtypeStruct((rows, wide + columns), jnp.bfloat16)] * peers,
        in_specs=[SMEM, VMEM, VMEM, VMEM],
        out_specs=[VMEM] * peers,
        scratch_shapes=[
            pltpu.VMEM((rows, features), jnp.float32),
            pltpu.VMEM((rows, wide), jnp.float32),
            pltpu.VMEM((peers, rows, wide), jnp.bfloat16),
        ],
        name="student",
        cost_estimate=cost(2 * rows * features * columns, 2 * features * columns),
    )(me, hidden, gain, projection)


def teacher_kernel(first_ref, second_ref, residual_ref, slots_ref, marks_ref, out_ref):
    rows, columns = residual_ref.shape
    half = columns // 2
    sums = []
    for terms_ref in (first_ref, second_ref):
        total = terms_ref[0].astype(jnp.float32)
        for k in range(1, terms_ref.shape[0]):
            total = total + terms_ref[k].astype(jnp.float32)
        sums.append(total)
    summed = jnp.concatenate(sums, axis=1)
    teacher = (residual_ref[...].astype(jnp.float32) + summed).astype(jnp.bfloat16)
    lines = lax.broadcasted_iota(jnp.int32, (out_ref.shape[0], rows), 0)
    full, low, high = (
        (lines == slots_ref[k : k + 1, :]).astype(jnp.float32).astype(jnp.bfloat16) for k in range(3)
    )

    def moved(select, part):
        return jnp.dot(select, part, preferred_element_type=jnp.float32)

    rest = moved(low, teacher[:, :half]) + moved(high, teacher[:, half:])
    out_ref[:, :columns] = moved(full, teacher).astype(jnp.bfloat16)
    out_ref[:, columns : columns + half] = rest.astype(jnp.bfloat16)
    out_ref[:, columns + half :] = moved(full + low + high, marks_ref[...]).astype(jnp.bfloat16)


def teacher_rows(first, second, residual, slots, marks, lines):
    rows, columns = residual.shape
    width = columns + columns // 2 + MARKS
    return pl.pallas_call(
        teacher_kernel,
        out_shape=jax.ShapeDtypeStruct((lines, width), jnp.bfloat16),
        in_specs=[VMEM] * 5,
        out_specs=VMEM,
        name="teacher_rows",
        cost_estimate=cost(2 * rows * width * lines, 16 * residual.size),
    )(first, second, residual, slots, marks)


def gradient_kernel(me_ref, rows_ref, *refs):
    student_refs, (sum_ref, max_ref) = refs[:-2], refs[-2:]
    height, columns = sum_ref.shape
    groups, per = len(student_refs), student_refs[0].shape[0]
    pred_at = lane_tiles(height)
    half = columns // 2
    lines, tokens = rows_ref.shape[0], groups * per
    marks = rows_ref[:, columns + half :].astype(jnp.float32).astype(jnp.int32)
    lanes = lax.broadcasted_iota(jnp.int32, (lines, tokens), 1)
    line = lax.broadcasted_iota(jnp.int32, (lines, tokens), 0)
    low_half = (line & (FULL - 1)) < REST

    def select(at, wanted):
        place = (marks[:, at : at + 1] ^ me_ref[0]) * per + marks[:, at + 1 : at + 2]
        return ((lanes == place) & wanted).astype(jnp.float32).astype(jnp.bfloat16)

    def placed(chosen, start):
        return lax.dot_general(
            chosen, rows_ref[:, start : start + half], ROWS_FIRST, preferred_element_type=jnp.float32
        )

    full = select(0, True)
    target = [
        placed(full, 0) + placed(select(2, low_half), columns),
        placed(full, half) + placed(select(2, ~low_half), columns),
    ]
    largest = jnp.zeros((1, 1), jnp.float32)
    for side in range(2):
        cols = slice(side * half, (side + 1) * half)
        total = None
        for g, ref in enumerate(student_refs):
            aimed = target[side][g * per : (g + 1) * per]
            pred = ref[:, pred_at + side * half : pred_at + (side + 1) * half]
            diff = (pred.astype(jnp.float32) - aimed).astype(jnp.bfloat16)
            part = lax.dot_general(
                ref[:, :height], diff, ROWS_FIRST, preferred_element_type=jnp.float32
            )
            largest = jnp.maximum(largest, jnp.max(jnp.abs(part), keepdims=True))
            total = part if total is None else total + part
        sum_ref[:, cols] = total.astype(jnp.bfloat16)
    max_ref[0, 0] = jnp.max(largest)


def gradient(me, rows, packed, height, columns):
    tokens = len(packed) * packed[0].shape[0]
    return pl.pallas_call(
        gradient_kernel,
        out_shape=(
            jax.ShapeDtypeStruct((height, columns), jnp.bfloat16),
            jax.ShapeDtypeStruct((1, 1), jnp.float32),
        ),
        in_specs=[SMEM, VMEM] + [VMEM] * len(packed),
        out_specs=(VMEM, SMEM),
        name="gradient",
        cost_estimate=cost(4 * tokens * height * columns, 4 * tokens * height),
    )(me, rows, *packed)


def per_device(student_hidden, norm_gain, projection, teacher_partials, teacher_residual, owner):
    rows_dev, columns = teacher_residual.shape
    features = student_hidden.shape[1]
    nx, nz, nc = (lax.axis_size(a) for a in (X, Z, C))
    peers = nx * nc
    block = features // (nx * nz * nc)
    assert rows_dev == nz * (FULL + REST)
    me = lax.axis_index(X) * nc + lax.axis_index(C)
    me_ref = me.reshape(1).astype(jnp.int32)

    partner = [(0, 1), (1, 0)]
    here = lax.axis_index(XH).reshape(1).astype(jnp.int32)
    own_terms = teacher_partials[0]
    starts = [start for start, _ in pieces_of(columns)]
    away = split_columns(1 - here, own_terms, lax.axis_size(Y), columns)
    early = lax.ppermute(away[0], XH, partner)
    late = lax.ppermute(away[1], XH, partner)

    packed = student(me_ref, student_hidden, norm_gain[None], projection, (nx, nz, nc, block))
    early = pair_sum(here, own_terms, early, starts[0], columns)
    early, packed = lax.optimization_barrier((early, packed))
    packed = [packed[0]] + [to_peer(packed[k], k) for k in range(1, peers)]
    first = exchange(early, (Y,))
    first, late = lax.optimization_barrier((first, late))
    late = pair_sum(here, own_terms, late, starts[1], columns)
    second = exchange(late, (Y,))

    whose = owner // rows_dev
    z_to = (whose // nc) % nz
    peer_to = (whose // (nz * nc)) * nc + whose % nc
    index = jnp.arange(rows_dev)
    earlier = (z_to[None, :] == z_to[:, None]) & (index[None, :] < index[:, None])
    rank = jnp.sum(earlier.astype(jnp.int32), axis=1)
    full = rank < FULL
    line = z_to * FULL + jnp.where(full, rank, rank - FULL)
    slots = jnp.stack([jnp.where(full, line, -1), jnp.where(full, -1, line)])
    slots = jnp.concatenate([slots, jnp.where(full, -1, line + REST)[None]])
    lane = lax.broadcasted_iota(jnp.int32, (rows_dev, MARKS), 1) - jnp.where(full, 0, 2)[:, None]
    marks = jnp.where(lane == 0, peer_to[:, None], (owner % rows_dev)[:, None])
    marks = jnp.where((lane == 0) | (lane == 1), marks, 0).astype(jnp.bfloat16)

    second, packed = lax.optimization_barrier((second, packed))

    outgoing = teacher_rows(first, second, teacher_residual, slots, marks, nz * FULL)
    arrived = exchange(outgoing.reshape(nz, FULL, -1), Z).reshape(nz * FULL, -1)
    rows = lax.all_gather(arrived, XC, axis=0, tiled=True)

    tile, largest = gradient(me_ref, rows, packed, nz * block, columns)
    pieces = exchange(tile.reshape(nz, block, columns), Z)
    scale = largest[0, 0]
    for axes in (C, (XH, X), Y, ZL, ZH):
        scale = lax.pmax(scale, axes)
    scale = scale + 1e-06
    return jnp.sum(pieces.astype(jnp.float32), axis=0) / scale


def solution(mesh):
    torus = Mesh(mesh.devices.reshape(2, 3, 4, 2, 2, 8), (X, ZH, ZL, C, XH, Y))
    placed = (P(DP, None), P(), P(None, TP), P(TP, DP, None), P(DP, TP), P(DP))
    return jax.shard_map(
        per_device, mesh=torus, in_specs=placed, out_specs=P(DP, TP), check_vma=False
    )
```

time: 173 us -> 192 us (1.11)
  the two profiles are of different devices: /device:TPU:24 before, /device:TPU:8 now
where the time goes in v3:
time: 192 us
  blocking collectives  109 us (57%)
  waiting for transfers between devices  32.9 us (17%)
  starting transfers between devices  23.5 us (12%)
  Pallas kernels  19.4 us (10%)
  local copies, waits for them, and re-layouts  3.27 us (2%)
  other arithmetic  2.41 us (1%)
    pmax x5, blocking collectives, per_device(): scale = lax.pmax(scale, axes)  54 us
    all_to_all x2, blocking collectives, exchange(): return lax.all_to_all(array, axes, split_axis=0, concat_axis=0, tiled=True)  46.8 us
    ppermute x1, waiting for transfers between devices, per_device(): early = lax.ppermute(away[0], XH, partner)  18.1 us
    ppermute x3, waiting for transfers between devices, to_peer(): return lax.ppermute(array, XC, [(p, p ^ k) for p in range(4)])  14.8 us
    all_to_all x2, starting transfers between devices, exchange(): return lax.all_to_all(array, axes, split_axis=0, concat_axis=0, tiled=True)  8.62 us
    all_gather x1, blocking collectives, per_device(): rows = lax.all_gather(arrived, XC, axis=0, tiled=True)  8.49 us
    ppermute x3, starting transfers between devices, to_peer(): return lax.ppermute(array, XC, [(p, p ^ k) for p in range(4)])  7.59 us
    pallas_call x1, Pallas kernels, student(): pl.pallas_call(lambda *refs: student_kernel(sizes, *refs), out_shape=[jax...  5.27 us
  transfers between devices with their start and end apart: 7, of which 3 were waited for; matrix products, arithmetic and copies ran while one was open for 1% of the time, Pallas kernels for 4%

profile of v3, /device:TPU:8, one launch (start us, length us, event | category | flops | bytes accessed | tf_op | source)
XLA Modules:
  0.0 191.6 jit_solution(10597886918110176855)
XLA Ops:
  0.0 0.0 copy-start.3
  0.0 2.4 %split_columns.1 = (bf16[8,144,128]{2,1,0:T(8,128)(2,1)}, bf16[8,144,384]{2,1,0:T(8,128)(2,1)}) custom-call(s32[1]{0:T(128)S(6)} %sub.28._, bf16[144,8192]{1,0:T(8,128)(2,1)} %bitcast.10), custom_call_target="tpu_custom_call" | custom-call | bytes 2359296 | tf_op jit(solution)/shard_map/split_columns/pallas_call | solution.py:49
  2.4 4.9 %collective-permute-start.1 = (bf16[8,144,384]{2,1,0:T(8,128)(2,1)}, bf16[8,144,384]{2,1,0:T(8,128)(2,1)S(1)}, u32[]{:S(2)}, u32[]{:S(2)}) collective-permute-start(bf16[8,144,384]{2,1,0:T(8,128)(2,1)} %get-tuple-element.31), channel_id=1, source_target_pairs={{0,8},{8,0},{1,9},{9,1},{2,10},{10,2},{3,11},{11,3},{4,12},{12,4},... | collective-permute-start | bytes 2654216 | tf_op jit(solution)/shard_map/ppermute | solution.py:245
  7.3 2.4 %collective-permute-start = (bf16[8,144,128]{2,1,0:T(8,128)(2,1)}, bf16[8,144,128]{2,1,0:T(8,128)(2,1)S(1)}, u32[]{:S(2)}, u32[]{:S(2)}) collective-permute-start(bf16[8,144,128]{2,1,0:T(8,128)(2,1)} %get-tuple-element.25), channel_id=1, source_target_pairs={{0,8},{8,0},{1,9},{9,1},{2,10},{10,2},{3,11},{11,3},{4,12},{12,4},... | collective-permute-start | bytes 884744 | tf_op jit(solution)/shard_map/ppermute | solution.py:244
  9.7 0.0 copy-done.3
  9.7 0.6 broadcast_in_dim.40.refs_2_
  10.3 5.3 %student.1 = (bf16[144,1408]{1,0:T(8,128)(2,1)}, bf16[144,1408]{1,0:T(8,128)(2,1)}, bf16[144,1408]{1,0:T(8,128)(2,1)}, bf16[144,1408]{1,0:T(8,128)(2,1)}) custom-call(s32[1]{0:T(128)} %bitcast.refs_0_.me_ref, bf16[144,3456]{1,0:T(8,128)(2,1)} %refs_1_.1, f32[1,3456]{1,0:T(1,128)} %broadcast_in_dim.40.refs_2_, bf16[3456,512]{1,0:T(8,128)(2,1)} %refs_3_.1), custom_call_target="tpu_custom_call" | custom-call | flops 509607936 | bytes 3538944 | tf_op jit(solution)/shard_map/student/pallas_call | solution.py:118
  15.6 18.1 %collective-permute-done.refs_2_ = bf16[8,144,128]{2,1,0:T(8,128)(2,1)S(1)} collective-permute-done((bf16[8,144,128]{2,1,0:T(8,128)(2,1)}, bf16[8,144,128]{2,1,0:T(8,128)(2,1)S(1)}, u32[]{:S(2)}, u32[]{:S(2)}) %collective-permute-start) | collective-permute-done | bytes 294944 | tf_op jit(solution)/shard_map/ppermute | solution.py:244
  33.7 0.0 copy-start.2
  33.7 0.7 copy-done.2
  34.4 2.1 %pair_sum.2 = bf16[8,144,128]{2,1,0:T(8,128)(2,1)} custom-call(s32[1]{0:T(128)} %bitcast.1.refs_0_, bf16[144,8192]{1,0:T(8,128)(2,1)} %bitcast.11, bf16[8,144,128]{2,1,0:T(8,128)(2,1)} %copy-done.2), custom_call_target="tpu_custom_call" | custom-call | flops 147456 | bytes 884736 | tf_op jit(solution)/shard_map/pair_sum/pallas_call | solution.py:72
  36.5 17.9 %all_to_all.20.first_ref = bf16[8,144,128]{2,1,0:T(8,128)(2,1)} all-to-all(bf16[8,144,128]{2,1,0:T(8,128)(2,1)} %pair_sum.2), channel_id=1, replica_groups=mesh['x_lo'=2,'z_hi'=3,'z_lo'=4,'core'=2,'x_hi'=2,'y'=8] {'y'}, dimensions={0} | all-to-all | bytes 589824 | tf_op jit(solution)/shard_map/all_to_all | solution.py:20
  54.4 0.0 copy-start.4
  54.4 0.0 copy-start.7
  54.4 0.0 copy-start.6
  54.4 0.0 copy-start.5
  54.4 0.0 collective-permute-done.1.refs_2_
  54.4 0.0 copy-start.1
  54.5 0.9 copy-done.1
  55.4 2.6 %pair_sum.3 = bf16[8,144,384]{2,1,0:T(8,128)(2,1)} custom-call(s32[1]{0:T(128)} %bitcast.1.refs_0_, bf16[144,8192]{1,0:T(8,128)(2,1)} %bitcast.12, bf16[8,144,384]{2,1,0:T(8,128)(2,1)} %copy-done.1), custom_call_target="tpu_custom_call" | custom-call | flops 442368 | bytes 2654208 | tf_op jit(solution)/shard_map/pair_sum/pallas_call | solution.py:72
  58.0 4.9 %all-to-all-start.1 = ((bf16[8,144,384]{2,1,0:T(8,128)(2,1)}), bf16[8,144,384]{2,1,0:T(8,128)(2,1)S(1)}, u32[]{:S(2)}, u32[]{:S(2)}) async-start(bf16[8,144,384]{2,1,0:T(8,128)(2,1)} %pair_sum.3), calls=%async_computation.1 | async-start | bytes 1769472 | tf_op jit(solution)/shard_map/all_to_all | solution.py:20
  63.0 0.0 copy-done.4
  63.0 0.2 convert_reduce_fusion.1
  63.2 0.0 copy-done.7
  63.2 1.9 %collective-permute-start.2 = (bf16[144,1408]{1,0:T(8,128)(2,1)S(1)}, bf16[144,1408]{1,0:T(8,128)(2,1)S(1)}, u32[]{:S(2)}, u32[]{:S(2)}) collective-permute-start(bf16[144,1408]{1,0:T(8,128)(2,1)S(1)} %copy-done.7), channel_id=1, source_target_pairs={{0,16},{16,0},{384,400},{400,384},{1,17},{17,1},{385,401},{401,385... | collective-permute-start | bytes 1216520 | tf_op jit(solution)/shard_map/ppermute | solution.py:24
  65.1 0.0 copy-done.6
  65.2 3.4 %collective-permute-start.3 = (bf16[144,1408]{1,0:T(8,128)(2,1)S(1)}, bf16[144,1408]{1,0:T(8,128)(2,1)S(1)}, u32[]{:S(2)}, u32[]{:S(2)}) collective-permute-start(bf16[144,1408]{1,0:T(8,128)(2,1)S(1)} %copy-done.6), channel_id=1, source_target_pairs={{0,384},{16,400},{384,0},{400,16},{1,385},{17,401},{385,1},{401,17... | collective-permute-start | bytes 1216520 | tf_op jit(solution)/shard_map/ppermute | solution.py:24
  68.6 0.0 copy-done.5
  68.6 2.3 %collective-permute-start.4 = (bf16[144,1408]{1,0:T(8,128)(2,1)S(1)}, bf16[144,1408]{1,0:T(8,128)(2,1)S(1)}, u32[]{:S(2)}, u32[]{:S(2)}) collective-permute-start(bf16[144,1408]{1,0:T(8,128)(2,1)S(1)} %copy-done.5), channel_id=1, source_target_pairs={{0,400},{16,384},{384,16},{400,0},{1,401},{17,385},{385,17},{401,1... | collective-permute-start | bytes 1216520 | tf_op jit(solution)/shard_map/ppermute | solution.py:24
  70.9 0.6 pad_add_fusion.slots_ref
  71.5 0.7 select_convert_fusion.marks_ref
  72.2 0.0 collective-permute-done.2.refs_1_
  72.2 0.0 copy-start.8
  72.2 7.1 %collective-permute-done.3.refs_2_ = bf16[144,1408]{1,0:T(8,128)(2,1)S(1)} collective-permute-done((bf16[144,1408]{1,0:T(8,128)(2,1)S(1)}, bf16[144,1408]{1,0:T(8,128)(2,1)S(1)}, u32[]{:S(2)}, u32[]{:S(2)}) %collective-permute-start.3) | collective-permute-done | bytes 405536 | tf_op jit(solution)/shard_map/ppermute | solution.py:24
  79.3 0.0 copy-start.9
  79.3 7.7 %collective-permute-done.4.refs_3_ = bf16[144,1408]{1,0:T(8,128)(2,1)S(1)} collective-permute-done((bf16[144,1408]{1,0:T(8,128)(2,1)S(1)}, bf16[144,1408]{1,0:T(8,128)(2,1)S(1)}, u32[]{:S(2)}, u32[]{:S(2)}) %collective-permute-start.4) | collective-permute-done | bytes 405536 | tf_op jit(solution)/shard_map/ppermute | solution.py:24
  87.0 0.0 copy-start.10
  87.0 0.0 all-to-all-done.1.second_ref
  87.0 0.0 copy-start
  87.0 1.0 copy-done
  88.0 2.3 %teacher_rows.1 = bf16[96,896]{1,0:T(8,128)(2,1)} custom-call(bf16[8,144,128]{2,1,0:T(8,128)(2,1)} %all_to_all.20.first_ref, bf16[8,144,384]{2,1,0:T(8,128)(2,1)} %copy-done, bf16[144,512]{1,0:T(8,128)(2,1)} %residual_ref.1, s32[3,144]{1,0:T(4,128)} %pad_add_fusion.slots_ref, bf16[144,128]{1,0:T(8,128)(2,1)} %select_convert_fusion.marks_ref), custom_call_target="tpu_custom_call" | custom-call | flops 24772608 | bytes 1179648 | tf_op jit(solution)/shard_map/teacher_rows/pallas_call | solution.py:161
  90.3 28.9 %all_to_all.21 = bf16[12,8,896]{2,1,0:T(8,128)(2,1)S(1)} all-to-all(bf16[12,8,896]{2,1,0:T(8,128)(2,1)} %bitcast.14), channel_id=1, replica_groups=mesh['x_lo'=2,'z_hi'=3,'z_lo'=4,'core'=2,'x_hi'=2,'y'=8] {'z_hi','z_lo'}, dimensions={0} | all-to-all | bytes 344064 | tf_op jit(solution)/shard_map/all_to_all | solution.py:20
  119.2 8.5 %all_gather.3.rows_ref = bf16[384,896]{1,0:T(8,128)(2,1)} all-gather(bf16[96,896]{1,0:T(8,128)(2,1)S(1)} %bitcast.15), channel_id=1, replica_groups=mesh['x_lo'=2,'z_hi'=3,'z_lo'=4,'core'=2,'x_hi'=2,'y'=8] {'x_lo','core'}, dimensions={0}, use_global_device_ids=true | all-gather | bytes 860160 | tf_op jit(solution)/shard_map/all_gather | solution.py:274
  127.7 0.0 copy-done.8
  127.7 0.0 copy-done.9
  127.7 0.0 copy-done.10
  127.7 4.7 %gradient.1 = (bf16[864,512]{1,0:T(8,128)(2,1)}, f32[1,1]{1,0:T(1,128)}) custom-call(s32[1]{0:T(128)} %bitcast.refs_0_.me_ref, bf16[384,896]{1,0:T(8,128)(2,1)} %all_gather.3.rows_ref, bf16[144,1408]{1,0:T(8,128)(2,1)} %get-tuple-element.39.refs_0_, bf16[144,1408]{1,0:T(8,128)(2,1)} %copy-done.8, bf16[144,1408]{1,0:T(8,128)(2,1)} %copy-done.9, ...), custom_call_target="tpu_custom_call" | custom-call | flops 1019215872 | bytes 1990656 | tf_op jit(solution)/shard_map/gradient/pallas_call | solution.py:216
  132.4 3.7 %all-to-all-start.3 = ((bf16[12,72,512]{2,1,0:T(8,128)(2,1)}), bf16[12,72,512]{2,1,0:T(8,128)(2,1)S(1)}, u32[]{:S(2)}, u32[]{:S(2)}) async-start(bf16[12,72,512]{2,1,0:T(8,128)(2,1)} %bitcast.13), calls=%async_computation.3 | async-start | bytes 1769472 | tf_op jit(solution)/shard_map/all_to_all | solution.py:20
  136.1 3.1 %pmax.35 = f32[]{:T(128)} all-reduce(f32[]{:T(128)} %bitcast.9), channel_id=1, replica_groups=mesh['x_lo'=2,'z_hi'=3,'z_lo'=4,'core'=2,'x_hi'=2,'y'=8] {'core'}, use_global_device_ids=true, to_apply=%region_2.3 | all-reduce | flops 1 | bytes 8 | tf_op jit(solution)/shard_map/pmax | solution.py:280
  139.2 10.4 %pmax.36 = f32[]{:T(128)} all-reduce(f32[]{:T(128)} %pmax.35), channel_id=1, replica_groups=mesh['x_lo'=2,'z_hi'=3,'z_lo'=4,'core'=2,'x_hi'=2,'y'=8] {'x_hi','x_lo'}, use_global_device_ids=true, to_apply=%region_3.4 | all-reduce | flops 1 | bytes 8 | tf_op jit(solution)/shard_map/pmax | solution.py:280
  149.6 16.3 %pmax.37 = f32[]{:T(128)} all-reduce(f32[]{:T(128)} %pmax.36), channel_id=1, replica_groups=mesh['x_lo'=2,'z_hi'=3,'z_lo'=4,'core'=2,'x_hi'=2,'y'=8] {'y'}, use_global_device_ids=true, to_apply=%region_4.5 | all-reduce | flops 1 | bytes 8 | tf_op jit(solution)/shard_map/pmax | solution.py:280
  165.9 12.6 %pmax.38 = f32[]{:T(128)} all-reduce(f32[]{:T(128)} %pmax.37), channel_id=1, replica_groups=mesh['x_lo'=2,'z_hi'=3,'z_lo'=4,'core'=2,'x_hi'=2,'y'=8] {'z_lo'}, use_global_device_ids=true, to_apply=%region_5.6 | all-reduce | flops 1 | bytes 8 | tf_op jit(solution)/shard_map/pmax | solution.py:280
  178.5 11.6 %pmax.39 = f32[]{:T(128)} all-reduce(f32[]{:T(128)} %pmax.38), channel_id=1, replica_groups=mesh['x_lo'=2,'z_hi'=3,'z_lo'=4,'core'=2,'x_hi'=2,'y'=8] {'z_hi'}, use_global_device_ids=true, to_apply=%region_6.7 | all-reduce | flops 1 | bytes 8 | tf_op jit(solution)/shard_map/pmax | solution.py:280
  190.8 0.0 all-to-all-done.3
  190.8 0.1 convert_reduce_fusion
  190.9 0.7 broadcast_divide_fusion
  (3 shorter events, 0.1 us)
Async XLA Ops:
  0.0 9.7 %copy-start.3 = (f32[3456]{0:T(1024)S(1)}, f32[3456]{0:T(1024)}, u32[]{:S(2)}) copy-start(f32[3456]{0:T(1024)} %param.7) | copy-start | bytes 41476
  2.4 52.1 %collective-permute-start.1 = (bf16[8,144,384]{2,1,0:T(8,128)(2,1)}, bf16[8,144,384]{2,1,0:T(8,128)(2,1)S(1)}, u32[]{:S(2)}, u32[]{:S(2)}) collective-permute-start(bf16[8,144,384]{2,1,0:T(8,128)(2,1)} %get-tuple-element.31), channel_id=1, source_target_pairs={{0,8},{8,0},{1,9},{9,1},{2,10},{10,2},{3,11},{11,3},{4,12},{12,4},... | collective-permute-start | bytes 2654216 | tf_op jit(solution)/shard_map/ppermute | solution.py:245
  7.3 26.4 %collective-permute-start = (bf16[8,144,128]{2,1,0:T(8,128)(2,1)}, bf16[8,144,128]{2,1,0:T(8,128)(2,1)S(1)}, u32[]{:S(2)}, u32[]{:S(2)}) collective-permute-start(bf16[8,144,128]{2,1,0:T(8,128)(2,1)} %get-tuple-element.25), channel_id=1, source_target_pairs={{0,8},{8,0},{1,9},{9,1},{2,10},{10,2},{3,11},{11,3},{4,12},{12,4},... | collective-permute-start | bytes 884744 | tf_op jit(solution)/shard_map/ppermute | solution.py:244
  33.7 0.7 copy-start.2
  54.4 8.5 %copy-start.4 = (s32[144]{0:T(256)S(1)}, s32[144]{0:T(256)}, u32[]{:S(2)}) copy-start(s32[144]{0:T(256)} %param.11) | copy-start | bytes 1732
  54.4 8.8 %copy-start.7 = (bf16[144,1408]{1,0:T(8,128)(2,1)S(1)}, bf16[144,1408]{1,0:T(8,128)(2,1)}, u32[]{:S(2)}) copy-start(bf16[144,1408]{1,0:T(8,128)(2,1)} %get-tuple-element.35) | copy-start | bytes 1216516
  54.4 10.7 %copy-start.6 = (bf16[144,1408]{1,0:T(8,128)(2,1)S(1)}, bf16[144,1408]{1,0:T(8,128)(2,1)}, u32[]{:S(2)}) copy-start(bf16[144,1408]{1,0:T(8,128)(2,1)} %get-tuple-element.36) | copy-start | bytes 1216516
  54.4 14.1 %copy-start.5 = (bf16[144,1408]{1,0:T(8,128)(2,1)S(1)}, bf16[144,1408]{1,0:T(8,128)(2,1)}, u32[]{:S(2)}) copy-start(bf16[144,1408]{1,0:T(8,128)(2,1)} %get-tuple-element.37) | copy-start | bytes 1216516
  54.4 1.0 copy-start.1
  58.0 29.0 %all-to-all-start.1 = ((bf16[8,144,384]{2,1,0:T(8,128)(2,1)}), bf16[8,144,384]{2,1,0:T(8,128)(2,1)S(1)}, u32[]{:S(2)}, u32[]{:S(2)}) async-start(bf16[8,144,384]{2,1,0:T(8,128)(2,1)} %pair_sum.3), calls=%async_computation.1 | async-start | bytes 1769472 | tf_op jit(solution)/shard_map/all_to_all | solution.py:20
  63.2 9.0 %collective-permute-start.2 = (bf16[144,1408]{1,0:T(8,128)(2,1)S(1)}, bf16[144,1408]{1,0:T(8,128)(2,1)S(1)}, u32[]{:S(2)}, u32[]{:S(2)}) collective-permute-start(bf16[144,1408]{1,0:T(8,128)(2,1)S(1)} %copy-done.7), channel_id=1, source_target_pairs={{0,16},{16,0},{384,400},{400,384},{1,17},{17,1},{385,401},{401,385... | collective-permute-start | bytes 1216520 | tf_op jit(solution)/shard_map/ppermute | solution.py:24
  65.2 14.1 %collective-permute-start.3 = (bf16[144,1408]{1,0:T(8,128)(2,1)S(1)}, bf16[144,1408]{1,0:T(8,128)(2,1)S(1)}, u32[]{:S(2)}, u32[]{:S(2)}) collective-permute-start(bf16[144,1408]{1,0:T(8,128)(2,1)S(1)} %copy-done.6), channel_id=1, source_target_pairs={{0,384},{16,400},{384,0},{400,16},{1,385},{17,401},{385,1},{401,17... | collective-permute-start | bytes 1216520 | tf_op jit(solution)/shard_map/ppermute | solution.py:24
  68.6 18.5 %collective-permute-start.4 = (bf16[144,1408]{1,0:T(8,128)(2,1)S(1)}, bf16[144,1408]{1,0:T(8,128)(2,1)S(1)}, u32[]{:S(2)}, u32[]{:S(2)}) collective-permute-start(bf16[144,1408]{1,0:T(8,128)(2,1)S(1)} %copy-done.5), channel_id=1, source_target_pairs={{0,400},{16,384},{384,16},{400,0},{1,401},{17,385},{385,17},{401,1... | collective-permute-start | bytes 1216520 | tf_op jit(solution)/shard_map/ppermute | solution.py:24
  72.2 55.5 %copy-start.8 = (bf16[144,1408]{1,0:T(8,128)(2,1)}, bf16[144,1408]{1,0:T(8,128)(2,1)S(1)}, u32[]{:S(2)}) copy-start(bf16[144,1408]{1,0:T(8,128)(2,1)S(1)} %collective-permute-done.2.refs_1_) | copy-start | bytes 1216516
  79.3 48.4 %copy-start.9 = (bf16[144,1408]{1,0:T(8,128)(2,1)}, bf16[144,1408]{1,0:T(8,128)(2,1)S(1)}, u32[]{:S(2)}) copy-start(bf16[144,1408]{1,0:T(8,128)(2,1)S(1)} %collective-permute-done.3.refs_2_) | copy-start | bytes 1216516
  87.0 40.7 %copy-start.10 = (bf16[144,1408]{1,0:T(8,128)(2,1)}, bf16[144,1408]{1,0:T(8,128)(2,1)S(1)}, u32[]{:S(2)}) copy-start(bf16[144,1408]{1,0:T(8,128)(2,1)S(1)} %collective-permute-done.4.refs_3_) | copy-start | bytes 1216516
  87.0 1.0 copy-start
  132.4 58.4 %all-to-all-start.3 = ((bf16[12,72,512]{2,1,0:T(8,128)(2,1)}), bf16[12,72,512]{2,1,0:T(8,128)(2,1)S(1)}, u32[]{:S(2)}, u32[]{:S(2)}) async-start(bf16[12,72,512]{2,1,0:T(8,128)(2,1)} %bitcast.13), calls=%async_computation.3 | async-start | bytes 1769472 | tf_op jit(solution)/shard_map/all_to_all | solution.py:20

commit v4 on v3

--- a/solution.py
+++ b/solution.py
@@ -32,45 +32,58 @@
     return pl.BlockSpec((array.shape[0], array.shape[1] // 2), lambda _, which: (0, which[0]))
 
 
-def pieces_of(columns):
-    return ((0, columns // 4), (columns // 4, columns))
-
-
-def split_kernel(_, in_ref, *out_refs):
-    columns = sum(ref.shape[-1] for ref in out_refs)
-    for ref, (start, stop) in zip(out_refs, pieces_of(columns)):
-        for k in range(ref.shape[0]):
-            ref[k] = in_ref[:, k * columns + start : k * columns + stop]
-
-
-def split_columns(which, array, parts, columns):
-    rows = array.shape[0]
-    shapes = [(parts, rows, stop - start) for start, stop in pieces_of(columns)]
-    return pl.pallas_call(
-        split_kernel,
-        out_shape=[jax.ShapeDtypeStruct(shape, array.dtype) for shape in shapes],
+def direct_kernel(in_ref, out_ref):
+    parts, _, width = out_ref.shape
+    for k in range(parts):
+        out_ref[k] = in_ref[:, 2 * k * width : (2 * k + 1) * width]
+
+
+def direct_columns(array, parts):
+    rows, width = array.shape
+    half = width // parts // 2
+    return pl.pallas_call(
+        direct_kernel,
+        out_shape=jax.ShapeDtypeStruct((parts, rows, half), array.dtype),
+        in_specs=[VMEM],
+        out_specs=VMEM,
+        name="direct_columns",
+        cost_estimate=cost(0, 3 * array.size),
+    )(array)
+
+
+def away_kernel(_, in_ref, out_ref):
+    parts, _, width = out_ref.shape
+    for k in range(parts):
+        out_ref[k] = in_ref[:, (2 * k + 1) * width : 2 * (k + 1) * width]
+
+
+def away_columns(which, array, parts):
+    rows, width = array.shape
+    shape = (parts, rows, width // parts // 4)
+    return pl.pallas_call(
+        away_kernel,
+        out_shape=jax.ShapeDtypeStruct(shape, array.dtype),
         grid_spec=pltpu.PrefetchScalarGridSpec(
             num_scalar_prefetch=1,
             grid=(1,),
             in_specs=[half_of(array)],
-            out_specs=[pl.BlockSpec(shape, lambda *_: (0, 0, 0)) for shape in shapes],
+            out_specs=pl.BlockSpec(shape, lambda *_: (0, 0, 0)),
         ),
-        name="split_columns",
+        name="away_columns",
         cost_estimate=cost(0, 2 * array.size),
     )(which, array)
 
 
-def pair_kernel(start, columns, _, in_ref, got_ref, out_ref):
-    width = got_ref.shape[-1]
-    for k in range(got_ref.shape[0]):
-        at = k * columns + start
-        mine = in_ref[:, at : at + width].astype(jnp.float32)
+def pair_kernel(_, in_ref, got_ref, out_ref):
+    parts, _, width = got_ref.shape
+    for k in range(parts):
+        mine = in_ref[:, (2 * k + 1) * width : 2 * (k + 1) * width].astype(jnp.float32)
         out_ref[k] = (mine + got_ref[k].astype(jnp.float32)).astype(jnp.bfloat16)
 
 
-def pair_sum(which, array, got, start, columns):
-    return pl.pallas_call(
-        lambda *refs: pair_kernel(start, columns, *refs),
+def pair_sum(which, array, got):
+    return pl.pallas_call(
+        pair_kernel,
         out_shape=jax.ShapeDtypeStruct(got.shape, got.dtype),
         grid_spec=pltpu.PrefetchScalarGridSpec(
             num_scalar_prefetch=1,
@@ -130,16 +143,24 @@
     )(me, hidden, gain, projection)
 
 
-def teacher_kernel(first_ref, second_ref, residual_ref, slots_ref, marks_ref, out_ref):
+def teacher_kernel(first_ref, second_ref, residual_ref, slots_ref, marks_ref, out_ref, late_ref, sems):
     rows, columns = residual_ref.shape
     half = columns // 2
-    sums = []
-    for terms_ref in (first_ref, second_ref):
-        total = terms_ref[0].astype(jnp.float32)
-        for k in range(1, terms_ref.shape[0]):
-            total = total + terms_ref[k].astype(jnp.float32)
-        sums.append(total)
-    summed = jnp.concatenate(sums, axis=1)
+    copies = [
+        pltpu.make_async_copy(second_ref.at[k], late_ref.at[k], sems.at[k])
+        for k in range(late_ref.shape[0])
+    ]
+    for copy in copies:
+        copy.start()
+    early = first_ref[0].astype(jnp.float32)
+    for k in range(1, first_ref.shape[0]):
+        early = early + first_ref[k].astype(jnp.float32)
+    for copy in copies:
+        copy.wait()
+    late = late_ref[0].astype(jnp.float32)
+    for k in range(1, late_ref.shape[0]):
+        late = late + late_ref[k].astype(jnp.float32)
+    summed = jnp.concatenate([early, late], axis=1)
     teacher = (residual_ref[...].astype(jnp.float32) + summed).astype(jnp.bfloat16)
     lines = lax.broadcasted_iota(jnp.int32, (out_ref.shape[0], rows), 0)
     full, low, high = (
@@ -161,8 +182,12 @@
     return pl.pallas_call(
         teacher_kernel,
         out_shape=jax.ShapeDtypeStruct((lines, width), jnp.bfloat16),
-        in_specs=[VMEM] * 5,
+        in_specs=[VMEM, pl.BlockSpec(memory_space=pl.ANY)] + [VMEM] * 3,
         out_specs=VMEM,
+        scratch_shapes=[
+            pltpu.VMEM(second.shape, second.dtype),
+            pltpu.SemaphoreType.DMA((second.shape[0],)),
+        ],
         name="teacher_rows",
         cost_estimate=cost(2 * rows * width * lines, 16 * residual.size),
     )(first, second, residual, slots, marks)
@@ -239,19 +264,16 @@
     partner = [(0, 1), (1, 0)]
     here = lax.axis_index(XH).reshape(1).astype(jnp.int32)
     own_terms = teacher_partials[0]
-    starts = [start for start, _ in pieces_of(columns)]
-    away = split_columns(1 - here, own_terms, lax.axis_size(Y), columns)
-    early = lax.ppermute(away[0], XH, partner)
-    late = lax.ppermute(away[1], XH, partner)
+    direct = direct_columns(own_terms, lax.axis_size(TP))
+    away = away_columns(1 - here, own_terms, lax.axis_size(Y))
+    first = exchange(direct, TP)
+    swapped = lax.ppermute(away, XH, partner)
 
     packed = student(me_ref, student_hidden, norm_gain[None], projection, (nx, nz, nc, block))
-    early = pair_sum(here, own_terms, early, starts[0], columns)
-    early, packed = lax.optimization_barrier((early, packed))
     packed = [packed[0]] + [to_peer(packed[k], k) for k in range(1, peers)]
-    first = exchange(early, (Y,))
-    first, late = lax.optimization_barrier((first, late))
-    late = pair_sum(here, own_terms, late, starts[1], columns)
-    second = exchange(late, (Y,))
+    paired = pair_sum(here, own_terms, swapped)
+    first, paired = lax.optimization_barrier((first, paired))
+    second = exchange(paired, (Y,))
 
     whose = owner // rows_dev
     z_to = (whose // nc) % nz

time: 192 us -> 174 us (0.906)
  blocking collectives: 109 us -> 90.1 us
  starting transfers between devices: 23.5 us -> 35.1 us
  waiting for transfers between devices: 32.9 us -> 21.7 us
    all_to_all x2 -> x1, blocking collectives: 46.8 us -> 28.1 us  [exchange(): return lax.all_to_all(array, axes, split_axis=0, concat_axis=0, tiled=True)]
    all_to_all x2 -> x3, starting transfers between devices: 8.62 us -> 22.6 us  [exchange(): return lax.all_to_all(array, axes, split_axis=0, concat_axis=0, tiled=True)]
    ppermute x3, waiting for transfers between devices: 14.8 us -> 1.22 us  [to_peer(): return lax.ppermute(array, XC, [(p, p ^ k) for p in range(4)])]
    all_to_all x2 -> x3, waiting for transfers between devices: 0.01 us -> 9.85 us  [exchange(): return lax.all_to_all(array, axes, split_axis=0, concat_axis=0, tiled=True)]
    ppermute x2 -> x1, waiting for transfers between devices: 18.1 us -> 10.7 us  [per_device(): swapped = lax.ppermute(away, XH, partner)]
    ppermute x2 -> x1, starting transfers between devices: 7.33 us -> 4.92 us  [per_device(): swapped = lax.ppermute(away, XH, partner)]
  transfers between devices with their start and end apart: 7 -> 7, of which waited for: 3 -> 3; matrix products, arithmetic and copies ran while one was open for 1% -> 1% of each run, Pallas kernels for 4% -> 6%
where the time goes in v4:
time: 174 us; the launch traced here: 173 us
  blocking collectives  90.1 us (52%)
  starting transfers between devices  35.1 us (20%)
  waiting for transfers between devices  21.7 us (12%)
  Pallas kernels  20.8 us (12%)
  other arithmetic  2.42 us (1%)
  local copies, waits for them, and re-layouts  2.33 us (1%)
    pmax x5, blocking collectives, per_device(): scale = lax.pmax(scale, axes)  54.4 us
    all_to_all x1, blocking collectives, exchange(): return lax.all_to_all(array, axes, split_axis=0, concat_axis=0, tiled=True)  28.1 us
    all_to_all x3, starting transfers between devices, exchange(): return lax.all_to_all(array, axes, split_axis=0, concat_axis=0, tiled=True)  22.6 us
    ppermute x1, waiting for transfers between devices, per_device(): swapped = lax.ppermute(away, XH, partner)  10.7 us
    all_to_all x3, waiting for transfers between devices, exchange(): return lax.all_to_all(array, axes, split_axis=0, concat_axis=0, tiled=True)  9.85 us
    all_gather x1, blocking collectives, per_device(): rows = lax.all_gather(arrived, XC, axis=0, tiled=True)  7.6 us
    ppermute x3, starting transfers between devices, to_peer(): return lax.ppermute(array, XC, [(p, p ^ k) for p in range(4)])  7.57 us
    pallas_call x1, Pallas kernels, student(): pl.pallas_call(lambda *refs: student_kernel(sizes, *refs), out_shape=[jax...  5.24 us
  transfers between devices with their start and end apart: 7, of which 3 were waited for; matrix products, arithmetic and copies ran while one was open for 1% of the time, Pallas kernels for 6%

profile of v4, /device:TPU:8, one launch (start us, length us, event | category | flops | bytes accessed | tf_op | source)
XLA Modules:
  0.0 173.2 jit_solution(1918201837700755883)
XLA Ops:
  0.0 2.8 %direct_columns.1 = bf16[16,144,256]{2,1,0:T(8,128)(2,1)} custom-call(bf16[144,8192]{1,0:T(8,128)(2,1)} %bitcast.10), custom_call_target="tpu_custom_call" | custom-call | bytes 3538944 | tf_op jit(solution)/shard_map/direct_columns/pallas_call | solution.py:44
  2.8 12.9 %all-to-all-start = ((bf16[16,144,256]{2,1,0:T(8,128)(2,1)}), bf16[16,144,256]{2,1,0:T(8,128)(2,1)S(1)}, u32[]{:S(2)}, u32[]{:S(2)}) async-start(bf16[16,144,256]{2,1,0:T(8,128)(2,1)} %direct_columns.1), calls=%async_computation | async-start | bytes 2359296 | tf_op jit(solution)/shard_map/all_to_all | solution.py:20
  15.7 0.0 copy-start.3
  15.7 2.2 %away_columns.1 = bf16[8,144,256]{2,1,0:T(8,128)(2,1)} custom-call(s32[1]{0:T(128)S(6)} %sub.28._, bf16[144,8192]{1,0:T(8,128)(2,1)} %bitcast.11), custom_call_target="tpu_custom_call" | custom-call | bytes 2359296 | tf_op jit(solution)/shard_map/away_columns/pallas_call | solution.py:63
  17.9 4.9 %collective-permute-start = (bf16[8,144,256]{2,1,0:T(8,128)(2,1)}, bf16[8,144,256]{2,1,0:T(8,128)(2,1)S(1)}, u32[]{:S(2)}, u32[]{:S(2)}) collective-permute-start(bf16[8,144,256]{2,1,0:T(8,128)(2,1)} %away_columns.1), channel_id=1, source_target_pairs={{0,8},{8,0},{1,9},{9,1},{2,10},{10,2},{3,11},{11,3},{4,12},{12,4},... | collective-permute-start | bytes 1769480 | tf_op jit(solution)/shard_map/ppermute | solution.py:270
  22.8 0.0 copy-done.3
  22.8 0.6 broadcast_in_dim.40.refs_2_
  23.4 5.2 %student.1 = (bf16[144,1408]{1,0:T(8,128)(2,1)}, bf16[144,1408]{1,0:T(8,128)(2,1)}, bf16[144,1408]{1,0:T(8,128)(2,1)}, bf16[144,1408]{1,0:T(8,128)(2,1)}) custom-call(s32[1]{0:T(128)} %bitcast.refs_0_.me_ref, bf16[144,3456]{1,0:T(8,128)(2,1)} %refs_1_.1, f32[1,3456]{1,0:T(1,128)} %broadcast_in_dim.40.refs_2_, bf16[3456,512]{1,0:T(8,128)(2,1)} %refs_3_.1), custom_call_target="tpu_custom_call" | custom-call | flops 509607936 | bytes 3538944 | tf_op jit(solution)/shard_map/student/pallas_call | solution.py:131
  28.7 1.9 %collective-permute-start.1 = (bf16[144,1408]{1,0:T(8,128)(2,1)}, bf16[144,1408]{1,0:T(8,128)(2,1)S(1)}, u32[]{:S(2)}, u32[]{:S(2)}) collective-permute-start(bf16[144,1408]{1,0:T(8,128)(2,1)} %get-tuple-element.21), channel_id=1, source_target_pairs={{0,16},{16,0},{384,400},{400,384},{1,17},{17,1},{385,401},{401,385... | collective-permute-start | bytes 1216520 | tf_op jit(solution)/shard_map/ppermute | solution.py:24
  30.6 1.9 %collective-permute-start.2 = (bf16[144,1408]{1,0:T(8,128)(2,1)}, bf16[144,1408]{1,0:T(8,128)(2,1)S(1)}, u32[]{:S(2)}, u32[]{:S(2)}) collective-permute-start(bf16[144,1408]{1,0:T(8,128)(2,1)} %get-tuple-element.22), channel_id=1, source_target_pairs={{0,384},{16,400},{384,0},{400,16},{1,385},{17,401},{385,1},{401,17... | collective-permute-start | bytes 1216520 | tf_op jit(solution)/shard_map/ppermute | solution.py:24
  32.5 0.0 copy-start.4
  32.5 3.7 %collective-permute-start.3 = (bf16[144,1408]{1,0:T(8,128)(2,1)}, bf16[144,1408]{1,0:T(8,128)(2,1)S(1)}, u32[]{:S(2)}, u32[]{:S(2)}) collective-permute-start(bf16[144,1408]{1,0:T(8,128)(2,1)} %get-tuple-element.23), channel_id=1, source_target_pairs={{0,400},{16,384},{384,16},{400,0},{1,401},{17,385},{385,17},{401,1... | collective-permute-start | bytes 1216520 | tf_op jit(solution)/shard_map/ppermute | solution.py:24
  36.3 10.7 %collective-permute-done.got_ref = bf16[8,144,256]{2,1,0:T(8,128)(2,1)S(1)} collective-permute-done((bf16[8,144,256]{2,1,0:T(8,128)(2,1)}, bf16[8,144,256]{2,1,0:T(8,128)(2,1)S(1)}, u32[]{:S(2)}, u32[]{:S(2)}) %collective-permute-start) | collective-permute-done | bytes 589856 | tf_op jit(solution)/shard_map/ppermute | solution.py:270
  46.9 0.0 copy-start.2
  46.9 0.8 copy-done.2
  47.8 2.4 %pair_sum.1 = bf16[8,144,256]{2,1,0:T(8,128)(2,1)} custom-call(s32[1]{0:T(128)} %bitcast.2._, bf16[144,8192]{1,0:T(8,128)(2,1)} %bitcast.12, bf16[8,144,256]{2,1,0:T(8,128)(2,1)} %copy-done.2), custom_call_target="tpu_custom_call" | custom-call | flops 294912 | bytes 1769472 | tf_op jit(solution)/shard_map/pair_sum/pallas_call | solution.py:85
  50.2 0.0 all-to-all-done.first_ref
  50.2 0.0 copy-start
  50.2 6.0 %all-to-all-start.1 = ((bf16[8,144,256]{2,1,0:T(8,128)(2,1)}), bf16[8,144,256]{2,1,0:T(8,128)(2,1)S(1)}, u32[]{:S(2)}, u32[]{:S(2)}) async-start(bf16[8,144,256]{2,1,0:T(8,128)(2,1)} %pair_sum.1), calls=%async_computation.1 | async-start | bytes 1179648 | tf_op jit(solution)/shard_map/all_to_all | solution.py:20
  56.2 0.0 copy-done.4
  56.2 0.2 convert_reduce_fusion.1
  56.4 0.6 pad_add_fusion.slots_ref
  57.1 0.7 select_convert_fusion.marks_ref
  57.8 0.0 collective-permute-done.1.refs_1_
  57.8 0.0 copy-start.5
  57.8 0.0 collective-permute-done.2.refs_2_
  57.8 0.0 copy-start.6
  57.8 1.2 collective-permute-done.3.refs_3_
  59.0 0.0 copy-start.7
  59.0 9.8 %all-to-all-done.1.second_ref = bf16[8,144,256]{2,1,0:T(8,128)(2,1)S(1)} async-done(((bf16[8,144,256]{2,1,0:T(8,128)(2,1)}), bf16[8,144,256]{2,1,0:T(8,128)(2,1)S(1)}, u32[]{:S(2)}, u32[]{:S(2)}) %all-to-all-start.1) | async-done | bytes 589856 | tf_op jit(solution)/shard_map/all_to_all | solution.py:20
  68.9 0.0 copy-start.1
  68.9 0.0 copy-done
  68.9 0.9 copy-done.1
  69.7 3.5 %teacher_rows.1 = bf16[96,896]{1,0:T(8,128)(2,1)} custom-call(bf16[16,144,256]{2,1,0:T(8,128)(2,1)} %copy-done, bf16[8,144,256]{2,1,0:T(8,128)(2,1)} %copy-done.1, bf16[144,512]{1,0:T(8,128)(2,1)} %residual_ref.1, s32[3,144]{1,0:T(4,128)} %pad_add_fusion.slots_ref, bf16[144,128]{1,0:T(8,128)(2,1)} %select_convert_fusion.marks_ref), custom_call_target="tpu_custom_call" | custom-call | flops 24772608 | bytes 1179648 | tf_op jit(solution)/shard_map/teacher_rows/pallas_call | solution.py:182
  73.3 28.1 %all_to_all.20 = bf16[12,8,896]{2,1,0:T(8,128)(2,1)S(1)} all-to-all(bf16[12,8,896]{2,1,0:T(8,128)(2,1)} %bitcast.15), channel_id=1, replica_groups=mesh['x_lo'=2,'z_hi'=3,'z_lo'=4,'core'=2,'x_hi'=2,'y'=8] {'z_hi','z_lo'}, dimensions={0} | all-to-all | bytes 344064 | tf_op jit(solution)/shard_map/all_to_all | solution.py:20
  101.4 7.6 %all_gather.3.rows_ref = bf16[384,896]{1,0:T(8,128)(2,1)} all-gather(bf16[96,896]{1,0:T(8,128)(2,1)S(1)} %bitcast.14), channel_id=1, replica_groups=mesh['x_lo'=2,'z_hi'=3,'z_lo'=4,'core'=2,'x_hi'=2,'y'=8] {'x_lo','core'}, dimensions={0}, use_global_device_ids=true | all-gather | bytes 860160 | tf_op jit(solution)/shard_map/all_gather | solution.py:296
  109.0 0.0 copy-done.5
  109.0 0.0 copy-done.6
  109.0 0.0 copy-done.7
  109.0 4.7 %gradient.1 = (bf16[864,512]{1,0:T(8,128)(2,1)}, f32[1,1]{1,0:T(1,128)}) custom-call(s32[1]{0:T(128)} %bitcast.refs_0_.me_ref, bf16[384,896]{1,0:T(8,128)(2,1)} %all_gather.3.rows_ref, bf16[144,1408]{1,0:T(8,128)(2,1)} %get-tuple-element.25.refs_0_, bf16[144,1408]{1,0:T(8,128)(2,1)} %copy-done.5, bf16[144,1408]{1,0:T(8,128)(2,1)} %copy-done.6, ...), custom_call_target="tpu_custom_call" | custom-call | flops 1019215872 | bytes 1990656 | tf_op jit(solution)/shard_map/gradient/pallas_call | solution.py:241
  113.7 3.7 %all-to-all-start.3 = ((bf16[12,72,512]{2,1,0:T(8,128)(2,1)}), bf16[12,72,512]{2,1,0:T(8,128)(2,1)S(1)}, u32[]{:S(2)}, u32[]{:S(2)}) async-start(bf16[12,72,512]{2,1,0:T(8,128)(2,1)} %bitcast.13), calls=%async_computation.3 | async-start | bytes 1769472 | tf_op jit(solution)/shard_map/all_to_all | solution.py:20
  117.4 3.1 %pmax.35 = f32[]{:T(128)} all-reduce(f32[]{:T(128)} %bitcast.9), channel_id=1, replica_groups=mesh['x_lo'=2,'z_hi'=3,'z_lo'=4,'core'=2,'x_hi'=2,'y'=8] {'core'}, use_global_device_ids=true, to_apply=%region_2.3 | all-reduce | flops 1 | bytes 8 | tf_op jit(solution)/shard_map/pmax | solution.py:302
  120.5 10.6 %pmax.36 = f32[]{:T(128)} all-reduce(f32[]{:T(128)} %pmax.35), channel_id=1, replica_groups=mesh['x_lo'=2,'z_hi'=3,'z_lo'=4,'core'=2,'x_hi'=2,'y'=8] {'x_hi','x_lo'}, use_global_device_ids=true, to_apply=%region_3.4 | all-reduce | flops 1 | bytes 8 | tf_op jit(solution)/shard_map/pmax | solution.py:302
  131.1 16.4 %pmax.37 = f32[]{:T(128)} all-reduce(f32[]{:T(128)} %pmax.36), channel_id=1, replica_groups=mesh['x_lo'=2,'z_hi'=3,'z_lo'=4,'core'=2,'x_hi'=2,'y'=8] {'y'}, use_global_device_ids=true, to_apply=%region_4.5 | all-reduce | flops 1 | bytes 8 | tf_op jit(solution)/shard_map/pmax | solution.py:302
  147.6 12.6 %pmax.38 = f32[]{:T(128)} all-reduce(f32[]{:T(128)} %pmax.37), channel_id=1, replica_groups=mesh['x_lo'=2,'z_hi'=3,'z_lo'=4,'core'=2,'x_hi'=2,'y'=8] {'z_lo'}, use_global_device_ids=true, to_apply=%region_5.6 | all-reduce | flops 1 | bytes 8 | tf_op jit(solution)/shard_map/pmax | solution.py:302
  160.2 11.6 %pmax.39 = f32[]{:T(128)} all-reduce(f32[]{:T(128)} %pmax.38), channel_id=1, replica_groups=mesh['x_lo'=2,'z_hi'=3,'z_lo'=4,'core'=2,'x_hi'=2,'y'=8] {'z_hi'}, use_global_device_ids=true, to_apply=%region_6.7 | all-reduce | flops 1 | bytes 8 | tf_op jit(solution)/shard_map/pmax | solution.py:302
  172.4 0.0 all-to-all-done.3
  172.4 0.1 convert_reduce_fusion
  172.5 0.7 broadcast_divide_fusion
  (3 shorter events, 0.1 us)
Async XLA Ops:
  2.8 47.4 %all-to-all-start = ((bf16[16,144,256]{2,1,0:T(8,128)(2,1)}), bf16[16,144,256]{2,1,0:T(8,128)(2,1)S(1)}, u32[]{:S(2)}, u32[]{:S(2)}) async-start(bf16[16,144,256]{2,1,0:T(8,128)(2,1)} %direct_columns.1), calls=%async_computation | async-start | bytes 2359296 | tf_op jit(solution)/shard_map/all_to_all | solution.py:20
  15.7 7.1 %copy-start.3 = (f32[3456]{0:T(1024)S(1)}, f32[3456]{0:T(1024)}, u32[]{:S(2)}) copy-start(f32[3456]{0:T(1024)} %param.7) | copy-start | bytes 41476
  17.9 29.1 %collective-permute-start = (bf16[8,144,256]{2,1,0:T(8,128)(2,1)}, bf16[8,144,256]{2,1,0:T(8,128)(2,1)S(1)}, u32[]{:S(2)}, u32[]{:S(2)}) collective-permute-start(bf16[8,144,256]{2,1,0:T(8,128)(2,1)} %away_columns.1), channel_id=1, source_target_pairs={{0,8},{8,0},{1,9},{9,1},{2,10},{10,2},{3,11},{11,3},{4,12},{12,4},... | collective-permute-start | bytes 1769480 | tf_op jit(solution)/shard_map/ppermute | solution.py:270
  28.7 29.1 %collective-permute-start.1 = (bf16[144,1408]{1,0:T(8,128)(2,1)}, bf16[144,1408]{1,0:T(8,128)(2,1)S(1)}, u32[]{:S(2)}, u32[]{:S(2)}) collective-permute-start(bf16[144,1408]{1,0:T(8,128)(2,1)} %get-tuple-element.21), channel_id=1, source_target_pairs={{0,16},{16,0},{384,400},{400,384},{1,17},{17,1},{385,401},{401,385... | collective-permute-start | bytes 1216520 | tf_op jit(solution)/shard_map/ppermute | solution.py:24
  30.6 27.2 %collective-permute-start.2 = (bf16[144,1408]{1,0:T(8,128)(2,1)}, bf16[144,1408]{1,0:T(8,128)(2,1)S(1)}, u32[]{:S(2)}, u32[]{:S(2)}) collective-permute-start(bf16[144,1408]{1,0:T(8,128)(2,1)} %get-tuple-element.22), channel_id=1, source_target_pairs={{0,384},{16,400},{384,0},{400,16},{1,385},{17,401},{385,1},{401,17... | collective-permute-start | bytes 1216520 | tf_op jit(solution)/shard_map/ppermute | solution.py:24
  32.5 23.7 %copy-start.4 = (s32[144]{0:T(256)S(1)}, s32[144]{0:T(256)}, u32[]{:S(2)}) copy-start(s32[144]{0:T(256)} %param.11) | copy-start | bytes 1732
  32.5 26.5 %collective-permute-start.3 = (bf16[144,1408]{1,0:T(8,128)(2,1)}, bf16[144,1408]{1,0:T(8,128)(2,1)S(1)}, u32[]{:S(2)}, u32[]{:S(2)}) collective-permute-start(bf16[144,1408]{1,0:T(8,128)(2,1)} %get-tuple-element.23), channel_id=1, source_target_pairs={{0,400},{16,384},{384,16},{400,0},{1,401},{17,385},{385,17},{401,1... | collective-permute-start | bytes 1216520 | tf_op jit(solution)/shard_map/ppermute | solution.py:24
  46.9 0.8 copy-start.2
  50.2 18.7 %copy-start = (bf16[16,144,256]{2,1,0:T(8,128)(2,1)}, bf16[16,144,256]{2,1,0:T(8,128)(2,1)S(1)}, u32[]{:S(2)}) copy-start(bf16[16,144,256]{2,1,0:T(8,128)(2,1)S(1)} %all-to-all-done.first_ref) | copy-start | bytes 3538948
  50.2 18.7 %all-to-all-start.1 = ((bf16[8,144,256]{2,1,0:T(8,128)(2,1)}), bf16[8,144,256]{2,1,0:T(8,128)(2,1)S(1)}, u32[]{:S(2)}, u32[]{:S(2)}) async-start(bf16[8,144,256]{2,1,0:T(8,128)(2,1)} %pair_sum.1), calls=%async_computation.1 | async-start | bytes 1179648 | tf_op jit(solution)/shard_map/all_to_all | solution.py:20
  57.8 51.2 %copy-start.5 = (bf16[144,1408]{1,0:T(8,128)(2,1)}, bf16[144,1408]{1,0:T(8,128)(2,1)S(1)}, u32[]{:S(2)}) copy-start(bf16[144,1408]{1,0:T(8,128)(2,1)S(1)} %collective-permute-done.1.refs_1_) | copy-start | bytes 1216516
  57.8 51.2 %copy-start.6 = (bf16[144,1408]{1,0:T(8,128)(2,1)}, bf16[144,1408]{1,0:T(8,128)(2,1)S(1)}, u32[]{:S(2)}) copy-start(bf16[144,1408]{1,0:T(8,128)(2,1)S(1)} %collective-permute-done.2.refs_2_) | copy-start | bytes 1216516
  59.0 50.0 %copy-start.7 = (bf16[144,1408]{1,0:T(8,128)(2,1)}, bf16[144,1408]{1,0:T(8,128)(2,1)S(1)}, u32[]{:S(2)}) copy-start(bf16[144,1408]{1,0:T(8,128)(2,1)S(1)} %collective-permute-done.3.refs_3_) | copy-start | bytes 1216516
  68.9 0.9 copy-start.1
  113.7 58.7 %all-to-all-start.3 = ((bf16[12,72,512]{2,1,0:T(8,128)(2,1)}), bf16[12,72,512]{2,1,0:T(8,128)(2,1)S(1)}, u32[]{:S(2)}, u32[]{:S(2)}) async-start(bf16[12,72,512]{2,1,0:T(8,128)(2,1)} %bitcast.13), calls=%async_computation.3 | async-start | bytes 1769472 | tf_op jit(solution)/shard_map/all_to_all | solution.py:20

commit v5 on v4

--- a/solution.py
+++ b/solution.py
@@ -270,7 +270,9 @@
     swapped = lax.ppermute(away, XH, partner)
 
     packed = student(me_ref, student_hidden, norm_gain[None], projection, (nx, nz, nc, block))
-    packed = [packed[0]] + [to_peer(packed[k], k) for k in range(1, peers)]
+    near = [to_peer(packed[k], k) for k in range(1, nc)]
+    far = [to_peer(packed[k], k) for k in range(nc, peers)]
+    packed = [packed[0]] + near + far
     paired = pair_sum(here, own_terms, swapped)
     first, paired = lax.optimization_barrier((first, paired))
     second = exchange(paired, (Y,))
@@ -293,7 +295,8 @@
 
     outgoing = teacher_rows(first, second, teacher_residual, slots, marks, nz * FULL)
     arrived = exchange(outgoing.reshape(nz, FULL, -1), Z).reshape(nz * FULL, -1)
-    rows = lax.all_gather(arrived, XC, axis=0, tiled=True)
+    rows = lax.all_gather(arrived, X, axis=0, tiled=True)
+    rows = lax.all_gather(rows, C, axis=0, tiled=True)
 
     tile, largest = gradient(me_ref, rows, packed, nz * block, columns)
     pieces = exchange(tile.reshape(nz, block, columns), Z)

time: 174 us -> 175 us (level)
    all_gather x1 -> x2, blocking collectives: 7.6 us -> 8.48 us  [the longest x1 6.06 us: per_device(): rows = lax.all_gather(arrived, X, axis=0, tiled=True)]
where the time goes in v5:
time: 175 us; the launch traced here: 174 us
  blocking collectives  90.7 us (52%)
  starting transfers between devices  35.1 us (20%)
  waiting for transfers between devices  21.7 us (12%)
  Pallas kernels  20.8 us (12%)
  other arithmetic  2.42 us (1%)
  local copies, waits for them, and re-layouts  2.33 us (1%)
    pmax x5, blocking collectives, per_device(): scale = lax.pmax(scale, axes)  54.1 us
    all_to_all x1, blocking collectives, exchange(): return lax.all_to_all(array, axes, split_axis=0, concat_axis=0, tiled=True)  28.1 us
    all_to_all x3, starting transfers between devices, exchange(): return lax.all_to_all(array, axes, split_axis=0, concat_axis=0, tiled=True)  22.6 us
    ppermute x1, waiting for transfers between devices, per_device(): swapped = lax.ppermute(away, XH, partner)  10.7 us
    all_to_all x3, waiting for transfers between devices, exchange(): return lax.all_to_all(array, axes, split_axis=0, concat_axis=0, tiled=True)  9.85 us
    ppermute x3, starting transfers between devices, to_peer(): return lax.ppermute(array, XC, [(p, p ^ k) for p in range(4)])  7.57 us
    all_gather x1, blocking collectives, per_device(): rows = lax.all_gather(arrived, X, axis=0, tiled=True)  6.06 us
    pallas_call x1, Pallas kernels, student(): pl.pallas_call(lambda *refs: student_kernel(sizes, *refs), out_shape=[jax...  5.24 us
  transfers between devices with their start and end apart: 7, of which 3 were waited for; matrix products, arithmetic and copies ran while one was open for 1% of the time, Pallas kernels for 6%

profile of v5, /device:TPU:8, one launch (start us, length us, event | category | flops | bytes accessed | tf_op | source)
XLA Modules:
  0.0 173.9 jit_solution(7992354205876123173)
XLA Ops:
  0.0 2.8 %direct_columns.1 = bf16[16,144,256]{2,1,0:T(8,128)(2,1)} custom-call(bf16[144,8192]{1,0:T(8,128)(2,1)} %bitcast.10), custom_call_target="tpu_custom_call" | custom-call | bytes 3538944 | tf_op jit(solution)/shard_map/direct_columns/pallas_call | solution.py:44
  2.8 12.9 %all-to-all-start = ((bf16[16,144,256]{2,1,0:T(8,128)(2,1)}), bf16[16,144,256]{2,1,0:T(8,128)(2,1)S(1)}, u32[]{:S(2)}, u32[]{:S(2)}) async-start(bf16[16,144,256]{2,1,0:T(8,128)(2,1)} %direct_columns.1), calls=%async_computation | async-start | bytes 2359296 | tf_op jit(solution)/shard_map/all_to_all | solution.py:20
  15.7 0.0 copy-start.3
  15.7 2.2 %away_columns.1 = bf16[8,144,256]{2,1,0:T(8,128)(2,1)} custom-call(s32[1]{0:T(128)S(6)} %sub.28._, bf16[144,8192]{1,0:T(8,128)(2,1)} %bitcast.11), custom_call_target="tpu_custom_call" | custom-call | bytes 2359296 | tf_op jit(solution)/shard_map/away_columns/pallas_call | solution.py:63
  17.9 4.9 %collective-permute-start = (bf16[8,144,256]{2,1,0:T(8,128)(2,1)}, bf16[8,144,256]{2,1,0:T(8,128)(2,1)S(1)}, u32[]{:S(2)}, u32[]{:S(2)}) collective-permute-start(bf16[8,144,256]{2,1,0:T(8,128)(2,1)} %away_columns.1), channel_id=1, source_target_pairs={{0,8},{8,0},{1,9},{9,1},{2,10},{10,2},{3,11},{11,3},{4,12},{12,4},... | collective-permute-start | bytes 1769480 | tf_op jit(solution)/shard_map/ppermute | solution.py:270
  22.8 0.0 copy-done.3
  22.8 0.6 broadcast_in_dim.40.refs_2_
  23.4 5.2 %student.1 = (bf16[144,1408]{1,0:T(8,128)(2,1)}, bf16[144,1408]{1,0:T(8,128)(2,1)}, bf16[144,1408]{1,0:T(8,128)(2,1)}, bf16[144,1408]{1,0:T(8,128)(2,1)}) custom-call(s32[1]{0:T(128)} %bitcast.refs_0_.me_ref, bf16[144,3456]{1,0:T(8,128)(2,1)} %refs_1_.1, f32[1,3456]{1,0:T(1,128)} %broadcast_in_dim.40.refs_2_, bf16[3456,512]{1,0:T(8,128)(2,1)} %refs_3_.1), custom_call_target="tpu_custom_call" | custom-call | flops 509607936 | bytes 3538944 | tf_op jit(solution)/shard_map/student/pallas_call | solution.py:131
  28.7 1.9 %collective-permute-start.1 = (bf16[144,1408]{1,0:T(8,128)(2,1)}, bf16[144,1408]{1,0:T(8,128)(2,1)S(1)}, u32[]{:S(2)}, u32[]{:S(2)}) collective-permute-start(bf16[144,1408]{1,0:T(8,128)(2,1)} %get-tuple-element.21), channel_id=1, source_target_pairs={{0,16},{16,0},{384,400},{400,384},{1,17},{17,1},{385,401},{401,385... | collective-permute-start | bytes 1216520 | tf_op jit(solution)/shard_map/ppermute | solution.py:24
  30.6 1.9 %collective-permute-start.2 = (bf16[144,1408]{1,0:T(8,128)(2,1)}, bf16[144,1408]{1,0:T(8,128)(2,1)S(1)}, u32[]{:S(2)}, u32[]{:S(2)}) collective-permute-start(bf16[144,1408]{1,0:T(8,128)(2,1)} %get-tuple-element.22), channel_id=1, source_target_pairs={{0,384},{16,400},{384,0},{400,16},{1,385},{17,401},{385,1},{401,17... | collective-permute-start | bytes 1216520 | tf_op jit(solution)/shard_map/ppermute | solution.py:24
  32.5 0.0 copy-start.4
  32.5 3.7 %collective-permute-start.3 = (bf16[144,1408]{1,0:T(8,128)(2,1)}, bf16[144,1408]{1,0:T(8,128)(2,1)S(1)}, u32[]{:S(2)}, u32[]{:S(2)}) collective-permute-start(bf16[144,1408]{1,0:T(8,128)(2,1)} %get-tuple-element.23), channel_id=1, source_target_pairs={{0,400},{16,384},{384,16},{400,0},{1,401},{17,385},{385,17},{401,1... | collective-permute-start | bytes 1216520 | tf_op jit(solution)/shard_map/ppermute | solution.py:24
  36.3 10.7 %collective-permute-done.got_ref = bf16[8,144,256]{2,1,0:T(8,128)(2,1)S(1)} collective-permute-done((bf16[8,144,256]{2,1,0:T(8,128)(2,1)}, bf16[8,144,256]{2,1,0:T(8,128)(2,1)S(1)}, u32[]{:S(2)}, u32[]{:S(2)}) %collective-permute-start) | collective-permute-done | bytes 589856 | tf_op jit(solution)/shard_map/ppermute | solution.py:270
  46.9 0.0 copy-start.2
  46.9 0.8 copy-done.2
  47.8 2.4 %pair_sum.1 = bf16[8,144,256]{2,1,0:T(8,128)(2,1)} custom-call(s32[1]{0:T(128)} %bitcast.2._, bf16[144,8192]{1,0:T(8,128)(2,1)} %bitcast.12, bf16[8,144,256]{2,1,0:T(8,128)(2,1)} %copy-done.2), custom_call_target="tpu_custom_call" | custom-call | flops 294912 | bytes 1769472 | tf_op jit(solution)/shard_map/pair_sum/pallas_call | solution.py:85
  50.2 0.0 all-to-all-done.first_ref
  50.2 0.0 copy-start
  50.2 6.0 %all-to-all-start.1 = ((bf16[8,144,256]{2,1,0:T(8,128)(2,1)}), bf16[8,144,256]{2,1,0:T(8,128)(2,1)S(1)}, u32[]{:S(2)}, u32[]{:S(2)}) async-start(bf16[8,144,256]{2,1,0:T(8,128)(2,1)} %pair_sum.1), calls=%async_computation.1 | async-start | bytes 1179648 | tf_op jit(solution)/shard_map/all_to_all | solution.py:20
  56.2 0.0 copy-done.4
  56.2 0.2 convert_reduce_fusion.1
  56.4 0.6 pad_add_fusion.slots_ref
  57.1 0.7 select_convert_fusion.marks_ref
  57.8 0.0 collective-permute-done.1.refs_1_
  57.8 0.0 copy-start.5
  57.8 0.0 collective-permute-done.2.refs_2_
  57.8 0.0 copy-start.6
  57.8 1.2 collective-permute-done.3.refs_3_
  59.0 0.0 copy-start.7
  59.0 9.8 %all-to-all-done.1.second_ref = bf16[8,144,256]{2,1,0:T(8,128)(2,1)S(1)} async-done(((bf16[8,144,256]{2,1,0:T(8,128)(2,1)}), bf16[8,144,256]{2,1,0:T(8,128)(2,1)S(1)}, u32[]{:S(2)}, u32[]{:S(2)}) %all-to-all-start.1) | async-done | bytes 589856 | tf_op jit(solution)/shard_map/all_to_all | solution.py:20
  68.9 0.0 copy-start.1
  68.9 0.0 copy-done
  68.9 0.9 copy-done.1
  69.7 3.5 %teacher_rows.1 = bf16[96,896]{1,0:T(8,128)(2,1)} custom-call(bf16[16,144,256]{2,1,0:T(8,128)(2,1)} %copy-done, bf16[8,144,256]{2,1,0:T(8,128)(2,1)} %copy-done.1, bf16[144,512]{1,0:T(8,128)(2,1)} %residual_ref.1, s32[3,144]{1,0:T(4,128)} %pad_add_fusion.slots_ref, bf16[144,128]{1,0:T(8,128)(2,1)} %select_convert_fusion.marks_ref), custom_call_target="tpu_custom_call" | custom-call | flops 24772608 | bytes 1179648 | tf_op jit(solution)/shard_map/teacher_rows/pallas_call | solution.py:182
  73.3 28.1 %all_to_all.20 = bf16[12,8,896]{2,1,0:T(8,128)(2,1)S(1)} all-to-all(bf16[12,8,896]{2,1,0:T(8,128)(2,1)} %bitcast.15), channel_id=1, replica_groups=mesh['x_lo'=2,'z_hi'=3,'z_lo'=4,'core'=2,'x_hi'=2,'y'=8] {'z_hi','z_lo'}, dimensions={0} | all-to-all | bytes 344064 | tf_op jit(solution)/shard_map/all_to_all | solution.py:20
  101.4 6.1 %all_gather.6 = bf16[192,896]{1,0:T(8,128)(2,1)S(1)} all-gather(bf16[96,896]{1,0:T(8,128)(2,1)S(1)} %bitcast.14), channel_id=1, replica_groups=mesh['x_lo'=2,'z_hi'=3,'z_lo'=4,'core'=2,'x_hi'=2,'y'=8] {'x_lo'}, dimensions={0}, use_global_device_ids=true | all-gather | bytes 516096 | tf_op jit(solution)/shard_map/all_gather | solution.py:298
  107.4 2.4 %all_gather.7.rows_ref = bf16[384,896]{1,0:T(8,128)(2,1)} all-gather(bf16[192,896]{1,0:T(8,128)(2,1)S(1)} %all_gather.6), channel_id=1, replica_groups=mesh['x_lo'=2,'z_hi'=3,'z_lo'=4,'core'=2,'x_hi'=2,'y'=8] {'core'}, dimensions={0}, use_global_device_ids=true | all-gather | bytes 1032192 | tf_op jit(solution)/shard_map/all_gather | solution.py:299
  109.9 0.0 copy-done.5
  109.9 0.0 copy-done.6
  109.9 0.0 copy-done.7
  109.9 4.7 %gradient.1 = (bf16[864,512]{1,0:T(8,128)(2,1)}, f32[1,1]{1,0:T(1,128)}) custom-call(s32[1]{0:T(128)} %bitcast.refs_0_.me_ref, bf16[384,896]{1,0:T(8,128)(2,1)} %all_gather.7.rows_ref, bf16[144,1408]{1,0:T(8,128)(2,1)} %get-tuple-element.25.refs_0_, bf16[144,1408]{1,0:T(8,128)(2,1)} %copy-done.5, bf16[144,1408]{1,0:T(8,128)(2,1)} %copy-done.6, ...), custom_call_target="tpu_custom_call" | custom-call | flops 1019215872 | bytes 1990656 | tf_op jit(solution)/shard_map/gradient/pallas_call | solution.py:241
  114.5 3.7 %all-to-all-start.3 = ((bf16[12,72,512]{2,1,0:T(8,128)(2,1)}), bf16[12,72,512]{2,1,0:T(8,128)(2,1)S(1)}, u32[]{:S(2)}, u32[]{:S(2)}) async-start(bf16[12,72,512]{2,1,0:T(8,128)(2,1)} %bitcast.13), calls=%async_computation.3 | async-start | bytes 1769472 | tf_op jit(solution)/shard_map/all_to_all | solution.py:20
  118.3 3.1 %pmax.35 = f32[]{:T(128)} all-reduce(f32[]{:T(128)} %bitcast.9), channel_id=1, replica_groups=mesh['x_lo'=2,'z_hi'=3,'z_lo'=4,'core'=2,'x_hi'=2,'y'=8] {'core'}, use_global_device_ids=true, to_apply=%region_2.3 | all-reduce | flops 1 | bytes 8 | tf_op jit(solution)/shard_map/pmax | solution.py:305
  121.4 10.4 %pmax.36 = f32[]{:T(128)} all-reduce(f32[]{:T(128)} %pmax.35), channel_id=1, replica_groups=mesh['x_lo'=2,'z_hi'=3,'z_lo'=4,'core'=2,'x_hi'=2,'y'=8] {'x_hi','x_lo'}, use_global_device_ids=true, to_apply=%region_3.4 | all-reduce | flops 1 | bytes 8 | tf_op jit(solution)/shard_map/pmax | solution.py:305
  131.7 16.4 %pmax.37 = f32[]{:T(128)} all-reduce(f32[]{:T(128)} %pmax.36), channel_id=1, replica_groups=mesh['x_lo'=2,'z_hi'=3,'z_lo'=4,'core'=2,'x_hi'=2,'y'=8] {'y'}, use_global_device_ids=true, to_apply=%region_4.5 | all-reduce | flops 1 | bytes 8 | tf_op jit(solution)/shard_map/pmax | solution.py:305
  148.2 12.6 %pmax.38 = f32[]{:T(128)} all-reduce(f32[]{:T(128)} %pmax.37), channel_id=1, replica_groups=mesh['x_lo'=2,'z_hi'=3,'z_lo'=4,'core'=2,'x_hi'=2,'y'=8] {'z_lo'}, use_global_device_ids=true, to_apply=%region_5.6 | all-reduce | flops 1 | bytes 8 | tf_op jit(solution)/shard_map/pmax | solution.py:305
  160.8 11.6 %pmax.39 = f32[]{:T(128)} all-reduce(f32[]{:T(128)} %pmax.38), channel_id=1, replica_groups=mesh['x_lo'=2,'z_hi'=3,'z_lo'=4,'core'=2,'x_hi'=2,'y'=8] {'z_hi'}, use_global_device_ids=true, to_apply=%region_6.7 | all-reduce | flops 1 | bytes 8 | tf_op jit(solution)/shard_map/pmax | solution.py:305
  173.1 0.0 all-to-all-done.3
  173.1 0.1 convert_reduce_fusion
  173.2 0.7 broadcast_divide_fusion
  (3 shorter events, 0.1 us)
Async XLA Ops:
  2.8 47.4 %all-to-all-start = ((bf16[16,144,256]{2,1,0:T(8,128)(2,1)}), bf16[16,144,256]{2,1,0:T(8,128)(2,1)S(1)}, u32[]{:S(2)}, u32[]{:S(2)}) async-start(bf16[16,144,256]{2,1,0:T(8,128)(2,1)} %direct_columns.1), calls=%async_computation | async-start | bytes 2359296 | tf_op jit(solution)/shard_map/all_to_all | solution.py:20
  15.7 7.1 %copy-start.3 = (f32[3456]{0:T(1024)S(1)}, f32[3456]{0:T(1024)}, u32[]{:S(2)}) copy-start(f32[3456]{0:T(1024)} %param.7) | copy-start | bytes 41476
  17.9 29.1 %collective-permute-start = (bf16[8,144,256]{2,1,0:T(8,128)(2,1)}, bf16[8,144,256]{2,1,0:T(8,128)(2,1)S(1)}, u32[]{:S(2)}, u32[]{:S(2)}) collective-permute-start(bf16[8,144,256]{2,1,0:T(8,128)(2,1)} %away_columns.1), channel_id=1, source_target_pairs={{0,8},{8,0},{1,9},{9,1},{2,10},{10,2},{3,11},{11,3},{4,12},{12,4},... | collective-permute-start | bytes 1769480 | tf_op jit(solution)/shard_map/ppermute | solution.py:270
  28.7 29.1 %collective-permute-start.1 = (bf16[144,1408]{1,0:T(8,128)(2,1)}, bf16[144,1408]{1,0:T(8,128)(2,1)S(1)}, u32[]{:S(2)}, u32[]{:S(2)}) collective-permute-start(bf16[144,1408]{1,0:T(8,128)(2,1)} %get-tuple-element.21), channel_id=1, source_target_pairs={{0,16},{16,0},{384,400},{400,384},{1,17},{17,1},{385,401},{401,385... | collective-permute-start | bytes 1216520 | tf_op jit(solution)/shard_map/ppermute | solution.py:24
  30.6 27.2 %collective-permute-start.2 = (bf16[144,1408]{1,0:T(8,128)(2,1)}, bf16[144,1408]{1,0:T(8,128)(2,1)S(1)}, u32[]{:S(2)}, u32[]{:S(2)}) collective-permute-start(bf16[144,1408]{1,0:T(8,128)(2,1)} %get-tuple-element.22), channel_id=1, source_target_pairs={{0,384},{16,400},{384,0},{400,16},{1,385},{17,401},{385,1},{401,17... | collective-permute-start | bytes 1216520 | tf_op jit(solution)/shard_map/ppermute | solution.py:24
  32.5 23.7 %copy-start.4 = (s32[144]{0:T(256)S(1)}, s32[144]{0:T(256)}, u32[]{:S(2)}) copy-start(s32[144]{0:T(256)} %param.11) | copy-start | bytes 1732
  32.5 26.5 %collective-permute-start.3 = (bf16[144,1408]{1,0:T(8,128)(2,1)}, bf16[144,1408]{1,0:T(8,128)(2,1)S(1)}, u32[]{:S(2)}, u32[]{:S(2)}) collective-permute-start(bf16[144,1408]{1,0:T(8,128)(2,1)} %get-tuple-element.23), channel_id=1, source_target_pairs={{0,400},{16,384},{384,16},{400,0},{1,401},{17,385},{385,17},{401,1... | collective-permute-start | bytes 1216520 | tf_op jit(solution)/shard_map/ppermute | solution.py:24
  46.9 0.8 copy-start.2
  50.2 18.7 %copy-start = (bf16[16,144,256]{2,1,0:T(8,128)(2,1)}, bf16[16,144,256]{2,1,0:T(8,128)(2,1)S(1)}, u32[]{:S(2)}) copy-start(bf16[16,144,256]{2,1,0:T(8,128)(2,1)S(1)} %all-to-all-done.first_ref) | copy-start | bytes 3538948
  50.2 18.7 %all-to-all-start.1 = ((bf16[8,144,256]{2,1,0:T(8,128)(2,1)}), bf16[8,144,256]{2,1,0:T(8,128)(2,1)S(1)}, u32[]{:S(2)}, u32[]{:S(2)}) async-start(bf16[8,144,256]{2,1,0:T(8,128)(2,1)} %pair_sum.1), calls=%async_computation.1 | async-start | bytes 1179648 | tf_op jit(solution)/shard_map/all_to_all | solution.py:20
  57.8 52.1 %copy-start.5 = (bf16[144,1408]{1,0:T(8,128)(2,1)}, bf16[144,1408]{1,0:T(8,128)(2,1)S(1)}, u32[]{:S(2)}) copy-start(bf16[144,1408]{1,0:T(8,128)(2,1)S(1)} %collective-permute-done.1.refs_1_) | copy-start | bytes 1216516
  57.8 52.1 %copy-start.6 = (bf16[144,1408]{1,0:T(8,128)(2,1)}, bf16[144,1408]{1,0:T(8,128)(2,1)S(1)}, u32[]{:S(2)}) copy-start(bf16[144,1408]{1,0:T(8,128)(2,1)S(1)} %collective-permute-done.2.refs_2_) | copy-start | bytes 1216516
  59.0 50.8 %copy-start.7 = (bf16[144,1408]{1,0:T(8,128)(2,1)}, bf16[144,1408]{1,0:T(8,128)(2,1)S(1)}, u32[]{:S(2)}) copy-start(bf16[144,1408]{1,0:T(8,128)(2,1)S(1)} %collective-permute-done.3.refs_3_) | copy-start | bytes 1216516
  68.9 0.9 copy-start.1
  114.5 58.5 %all-to-all-start.3 = ((bf16[12,72,512]{2,1,0:T(8,128)(2,1)}), bf16[12,72,512]{2,1,0:T(8,128)(2,1)S(1)}, u32[]{:S(2)}, u32[]{:S(2)}) async-start(bf16[12,72,512]{2,1,0:T(8,128)(2,1)} %bitcast.13), calls=%async_computation.3 | async-start | bytes 1769472 | tf_op jit(solution)/shard_map/all_to_all | solution.py:20

commit v6 on v4

--- a/solution.py
+++ b/solution.py
@@ -34,21 +34,52 @@
 
 def direct_kernel(in_ref, out_ref):
     parts, _, width = out_ref.shape
-    for k in range(parts):
-        out_ref[k] = in_ref[:, 2 * k * width : (2 * k + 1) * width]
+    half = width // 2
+    for side in range(2):
+        for k in range(parts):
+            start = (side * parts + k) * width
+            out_ref[k, :, side * half : (side + 1) * half] = in_ref[:, start : start + half]
 
 
 def direct_columns(array, parts):
     rows, width = array.shape
-    half = width // parts // 2
     return pl.pallas_call(
         direct_kernel,
-        out_shape=jax.ShapeDtypeStruct((parts, rows, half), array.dtype),
+        out_shape=jax.ShapeDtypeStruct((parts, rows, width // parts // 2), array.dtype),
         in_specs=[VMEM],
         out_specs=VMEM,
         name="direct_columns",
         cost_estimate=cost(0, 3 * array.size),
     )(array)
+
+
+def half_sum_kernel(here_ref, terms_ref, keep_ref, send_ref, total_ref):
+    total = terms_ref[0].astype(jnp.float32)
+    for k in range(1, terms_ref.shape[0]):
+        total = total + terms_ref[k].astype(jnp.float32)
+    total_ref[...] = total
+    half = keep_ref.shape[-1]
+    mine = pl.multiple_of(here_ref[0] * half, half)
+    other = pl.multiple_of((1 - here_ref[0]) * half, half)
+    keep_ref[...] = total_ref[:, pl.ds(mine, half)]
+    send_ref[...] = total_ref[:, pl.ds(other, half)].astype(jnp.bfloat16)
+
+
+def half_sum(here, terms):
+    _, rows, width = terms.shape
+    shape = (rows, width // 2)
+    return pl.pallas_call(
+        half_sum_kernel,
+        out_shape=(
+            jax.ShapeDtypeStruct(shape, jnp.float32),
+            jax.ShapeDtypeStruct(shape, jnp.bfloat16),
+        ),
+        in_specs=[SMEM, VMEM],
+        out_specs=(VMEM, VMEM),
+        scratch_shapes=[pltpu.VMEM((rows, width), jnp.float32)],
+        name="half_sum",
+        cost_estimate=cost(terms.size, 2 * terms.size),
+    )(here, terms)
 
 
 def away_kernel(_, in_ref, out_ref):
@@ -143,7 +174,7 @@
     )(me, hidden, gain, projection)
 
 
-def teacher_kernel(first_ref, second_ref, residual_ref, slots_ref, marks_ref, out_ref, late_ref, sems):
+def teacher_kernel(keep_ref, got_ref, second_ref, residual_ref, slots_ref, marks_ref, out_ref, late_ref, sems):
     rows, columns = residual_ref.shape
     half = columns // 2
     copies = [
@@ -152,9 +183,7 @@
     ]
     for copy in copies:
         copy.start()
-    early = first_ref[0].astype(jnp.float32)
-    for k in range(1, first_ref.shape[0]):
-        early = early + first_ref[k].astype(jnp.float32)
+    early = keep_ref[...] + got_ref[...].astype(jnp.float32)
     for copy in copies:
         copy.wait()
     late = late_ref[0].astype(jnp.float32)
@@ -176,13 +205,13 @@
     out_ref[:, columns + half :] = moved(full + low + high, marks_ref[...]).astype(jnp.bfloat16)
 
 
-def teacher_rows(first, second, residual, slots, marks, lines):
+def teacher_rows(keep, got, second, residual, slots, marks, lines):
     rows, columns = residual.shape
     width = columns + columns // 2 + MARKS
     return pl.pallas_call(
         teacher_kernel,
         out_shape=jax.ShapeDtypeStruct((lines, width), jnp.bfloat16),
-        in_specs=[VMEM, pl.BlockSpec(memory_space=pl.ANY)] + [VMEM] * 3,
+        in_specs=[VMEM, VMEM, pl.BlockSpec(memory_space=pl.ANY)] + [VMEM] * 3,
         out_specs=VMEM,
         scratch_shapes=[
             pltpu.VMEM(second.shape, second.dtype),
@@ -190,7 +219,7 @@
         ],
         name="teacher_rows",
         cost_estimate=cost(2 * rows * width * lines, 16 * residual.size),
-    )(first, second, residual, slots, marks)
+    )(keep, got, second, residual, slots, marks)
 
 
 def gradient_kernel(me_ref, rows_ref, *refs):
@@ -264,9 +293,9 @@
     partner = [(0, 1), (1, 0)]
     here = lax.axis_index(XH).reshape(1).astype(jnp.int32)
     own_terms = teacher_partials[0]
-    direct = direct_columns(own_terms, lax.axis_size(TP))
+    direct = direct_columns(own_terms, lax.axis_size(Y))
     away = away_columns(1 - here, own_terms, lax.axis_size(Y))
-    first = exchange(direct, TP)
+    first = exchange(direct, (Y,))
     swapped = lax.ppermute(away, XH, partner)
 
     packed = student(me_ref, student_hidden, norm_gain[None], projection, (nx, nz, nc, block))
@@ -274,6 +303,8 @@
     paired = pair_sum(here, own_terms, swapped)
     first, paired = lax.optimization_barrier((first, paired))
     second = exchange(paired, (Y,))
+    keep, send = half_sum(here, first)
+    got = lax.ppermute(send, XH, partner)
 
     whose = owner // rows_dev
     z_to = (whose // nc) % nz
@@ -289,9 +320,9 @@
     marks = jnp.where(lane == 0, peer_to[:, None], (owner % rows_dev)[:, None])
     marks = jnp.where((lane == 0) | (lane == 1), marks, 0).astype(jnp.bfloat16)
 
-    second, packed = lax.optimization_barrier((second, packed))
-
-    outgoing = teacher_rows(first, second, teacher_residual, slots, marks, nz * FULL)
+    second, packed, got = lax.optimization_barrier((second, packed, got))
+
+    outgoing = teacher_rows(keep, got, second, teacher_residual, slots, marks, nz * FULL)
     arrived = exchange(outgoing.reshape(nz, FULL, -1), Z).reshape(nz * FULL, -1)
     rows = lax.all_gather(arrived, XC, axis=0, tiled=True)
 

time: 174 us -> 169 us (0.971)
  waiting for transfers between devices: 21.7 us -> 11.5 us
  blocking collectives: 90.1 us -> 92.8 us
  Pallas kernels: 20.8 us -> 22.6 us
    ppermute x1, waiting for transfers between devices: 10.7 us -> 0.01 us  [per_device(): swapped = lax.ppermute(away, XH, partner)]
    ppermute x0 -> x1, starting transfers between devices: none -> 4.92 us  [per_device(): got = lax.ppermute(send, XH, partner)]
    ppermute x1, starting transfers between devices: 4.92 us -> 1.91 us  [per_device(): swapped = lax.ppermute(away, XH, partner)]
    ppermute x0 -> x1, waiting for transfers between devices: none -> 2.4 us  [per_device(): got = lax.ppermute(send, XH, partner)]
    pallas_call x0 -> x1, Pallas kernels: none -> 2.16 us  [half_sum(): pl.pallas_call(half_sum_kernel, out_shape=(jax.ShapeDtypeStruct(shape, jn...]
  transfers between devices with their start and end apart: 7 -> 8, of which waited for: 3 -> 3; matrix products, arithmetic and copies ran while one was open for 1% -> 1% of each run, Pallas kernels for 6% -> 7%
where the time goes in v6:
time: 169 us; the launch traced here: 168 us
  blocking collectives  92.8 us (55%)
  starting transfers between devices  36 us (21%)
  Pallas kernels  22.6 us (13%)
  waiting for transfers between devices  11.5 us (7%)
  other arithmetic  2.4 us (1%)
  local copies, waits for them, and re-layouts  2.3 us (1%)
    pmax x5, blocking collectives, per_device(): scale = lax.pmax(scale, axes)  55 us
    all_to_all x1, blocking collectives, exchange(): return lax.all_to_all(array, axes, split_axis=0, concat_axis=0, tiled=True)  29.3 us
    all_to_all x3, starting transfers between devices, exchange(): return lax.all_to_all(array, axes, split_axis=0, concat_axis=0, tiled=True)  21.6 us
    all_to_all x3, waiting for transfers between devices, exchange(): return lax.all_to_all(array, axes, split_axis=0, concat_axis=0, tiled=True)  9.05 us
    all_gather x1, blocking collectives, per_device(): rows = lax.all_gather(arrived, XC, axis=0, tiled=True)  8.5 us
    ppermute x3, starting transfers between devices, to_peer(): return lax.ppermute(array, XC, [(p, p ^ k) for p in range(4)])  7.57 us
    pallas_call x1, Pallas kernels, student(): pl.pallas_call(lambda *refs: student_kernel(sizes, *refs), out_shape=[jax...  5.23 us
    ppermute x1, starting transfers between devices, per_device(): got = lax.ppermute(send, XH, partner)  4.92 us
  transfers between devices with their start and end apart: 8, of which 3 were waited for; matrix products, arithmetic and copies ran while one was open for 1% of the time, Pallas kernels for 7%

profile of v6, /device:TPU:8, one launch (start us, length us, event | category | flops | bytes accessed | tf_op | source)
XLA Modules:
  0.0 168.3 jit_solution(15741349899017392777)
XLA Ops:
  0.0 2.8 %direct_columns.1 = bf16[8,144,512]{2,1,0:T(8,128)(2,1)} custom-call(bf16[144,8192]{1,0:T(8,128)(2,1)} %bitcast.10), custom_call_target="tpu_custom_call" | custom-call | bytes 3538944 | tf_op jit(solution)/shard_map/direct_columns/pallas_call | solution.py:46
  2.8 12.9 %all-to-all-start = ((bf16[8,144,512]{2,1,0:T(8,128)(2,1)}), bf16[8,144,512]{2,1,0:T(8,128)(2,1)S(1)}, u32[]{:S(2)}, u32[]{:S(2)}) async-start(bf16[8,144,512]{2,1,0:T(8,128)(2,1)} %direct_columns.1), calls=%async_computation | async-start | bytes 2359296 | tf_op jit(solution)/shard_map/all_to_all | solution.py:20
  15.7 0.0 copy-start.4
  15.7 2.2 %away_columns.1 = bf16[8,144,256]{2,1,0:T(8,128)(2,1)} custom-call(s32[1]{0:T(128)S(6)} %sub.28._, bf16[144,8192]{1,0:T(8,128)(2,1)} %bitcast.11), custom_call_target="tpu_custom_call" | custom-call | bytes 2359296 | tf_op jit(solution)/shard_map/away_columns/pallas_call | solution.py:94
  17.9 1.9 %collective-permute-start = (bf16[8,144,256]{2,1,0:T(8,128)(2,1)}, bf16[8,144,256]{2,1,0:T(8,128)(2,1)S(1)}, u32[]{:S(2)}, u32[]{:S(2)}) collective-permute-start(bf16[8,144,256]{2,1,0:T(8,128)(2,1)} %away_columns.1), channel_id=1, source_target_pairs={{0,8},{8,0},{1,9},{9,1},{2,10},{10,2},{3,11},{11,3},{4,12},{12,4},... | collective-permute-start | bytes 1769480 | tf_op jit(solution)/shard_map/ppermute | solution.py:299
  19.8 0.0 copy-done.4
  19.8 0.6 broadcast_in_dim.40.refs_2_
  20.4 5.2 %student.1 = (bf16[144,1408]{1,0:T(8,128)(2,1)}, bf16[144,1408]{1,0:T(8,128)(2,1)}, bf16[144,1408]{1,0:T(8,128)(2,1)}, bf16[144,1408]{1,0:T(8,128)(2,1)}) custom-call(s32[1]{0:T(128)} %bitcast.refs_0_.me_ref, bf16[144,3456]{1,0:T(8,128)(2,1)} %refs_1_.1, f32[1,3456]{1,0:T(1,128)} %broadcast_in_dim.40.refs_2_, bf16[3456,512]{1,0:T(8,128)(2,1)} %refs_3_.1), custom_call_target="tpu_custom_call" | custom-call | flops 509607936 | bytes 3538944 | tf_op jit(solution)/shard_map/student/pallas_call | solution.py:162
  25.6 1.9 %collective-permute-start.1 = (bf16[144,1408]{1,0:T(8,128)(2,1)}, bf16[144,1408]{1,0:T(8,128)(2,1)S(1)}, u32[]{:S(2)}, u32[]{:S(2)}) collective-permute-start(bf16[144,1408]{1,0:T(8,128)(2,1)} %get-tuple-element.25), channel_id=1, source_target_pairs={{0,16},{16,0},{384,400},{400,384},{1,17},{17,1},{385,401},{401,385... | collective-permute-start | bytes 1216520 | tf_op jit(solution)/shard_map/ppermute | solution.py:24
  27.5 1.9 %collective-permute-start.2 = (bf16[144,1408]{1,0:T(8,128)(2,1)}, bf16[144,1408]{1,0:T(8,128)(2,1)S(1)}, u32[]{:S(2)}, u32[]{:S(2)}) collective-permute-start(bf16[144,1408]{1,0:T(8,128)(2,1)} %get-tuple-element.26), channel_id=1, source_target_pairs={{0,384},{16,400},{384,0},{400,16},{1,385},{17,401},{385,1},{401,17... | collective-permute-start | bytes 1216520 | tf_op jit(solution)/shard_map/ppermute | solution.py:24
  29.5 0.0 copy-start.5
  29.5 3.7 %collective-permute-start.3 = (bf16[144,1408]{1,0:T(8,128)(2,1)}, bf16[144,1408]{1,0:T(8,128)(2,1)S(1)}, u32[]{:S(2)}, u32[]{:S(2)}) collective-permute-start(bf16[144,1408]{1,0:T(8,128)(2,1)} %get-tuple-element.27), channel_id=1, source_target_pairs={{0,400},{16,384},{384,16},{400,0},{1,401},{17,385},{385,17},{401,1... | collective-permute-start | bytes 1216520 | tf_op jit(solution)/shard_map/ppermute | solution.py:24
  33.2 0.0 collective-permute-done.got_ref
  33.2 0.0 copy-start.2
  33.3 0.8 copy-done.2
  34.1 2.4 %pair_sum.1 = bf16[8,144,256]{2,1,0:T(8,128)(2,1)} custom-call(s32[1]{0:T(128)} %bitcast.1._.here_ref, bf16[144,8192]{1,0:T(8,128)(2,1)} %bitcast.12, bf16[8,144,256]{2,1,0:T(8,128)(2,1)} %copy-done.2), custom_call_target="tpu_custom_call" | custom-call | flops 294912 | bytes 1769472 | tf_op jit(solution)/shard_map/pair_sum/pallas_call | solution.py:116
  36.5 3.9 %all-to-all-done.terms_ref = bf16[8,144,512]{2,1,0:T(8,128)(2,1)S(1)} async-done(((bf16[8,144,512]{2,1,0:T(8,128)(2,1)}), bf16[8,144,512]{2,1,0:T(8,128)(2,1)S(1)}, u32[]{:S(2)}, u32[]{:S(2)}) %all-to-all-start) | async-done | bytes 1179680 | tf_op jit(solution)/shard_map/all_to_all | solution.py:20
  40.4 0.0 copy-start
  40.4 4.9 %all-to-all-start.1 = ((bf16[8,144,256]{2,1,0:T(8,128)(2,1)}), bf16[8,144,256]{2,1,0:T(8,128)(2,1)S(1)}, u32[]{:S(2)}, u32[]{:S(2)}) async-start(bf16[8,144,256]{2,1,0:T(8,128)(2,1)} %pair_sum.1), calls=%async_computation.1 | async-start | bytes 1179648 | tf_op jit(solution)/shard_map/all_to_all | solution.py:20
  45.4 0.0 copy-done.5
  45.4 0.2 convert_reduce_fusion.1
  45.6 0.7 select_convert_fusion.marks_ref
  46.4 0.0 copy-done
  46.4 2.2 %half_sum.1 = (f32[144,256]{1,0:T(8,128)}, bf16[144,256]{1,0:T(8,128)(2,1)}) custom-call(s32[1]{0:T(128)} %bitcast.1._.here_ref, bf16[8,144,512]{2,1,0:T(8,128)(2,1)} %copy-done), custom_call_target="tpu_custom_call" | custom-call | flops 589824 | bytes 1179648 | tf_op jit(solution)/shard_map/half_sum/pallas_call | solution.py:71
  48.5 4.9 %collective-permute-start.4 = (bf16[144,256]{1,0:T(8,128)(2,1)}, bf16[144,256]{1,0:T(8,128)(2,1)S(1)}, u32[]{:S(2)}, u32[]{:S(2)}) collective-permute-start(bf16[144,256]{1,0:T(8,128)(2,1)} %get-tuple-element.28), channel_id=1, source_target_pairs={{0,8},{8,0},{1,9},{9,1},{2,10},{10,2},{3,11},{11,3},{4,12},{12,4},... | collective-permute-start | bytes 221192 | tf_op jit(solution)/shard_map/ppermute | solution.py:307
  53.5 0.6 pad_add_fusion.slots_ref
  54.1 0.0 collective-permute-done.1.refs_1_
  54.1 0.0 copy-start.6
  54.1 0.0 collective-permute-done.2.refs_2_
  54.1 0.0 copy-start.7
  54.1 0.0 collective-permute-done.3.refs_3_
  54.1 0.0 copy-start.8
  54.1 2.4 %collective-permute-done.4.got_ref = bf16[144,256]{1,0:T(8,128)(2,1)S(1)} collective-permute-done((bf16[144,256]{1,0:T(8,128)(2,1)}, bf16[144,256]{1,0:T(8,128)(2,1)S(1)}, u32[]{:S(2)}, u32[]{:S(2)}) %collective-permute-start.4) | collective-permute-done | bytes 73760 | tf_op jit(solution)/shard_map/ppermute | solution.py:307
  56.5 0.0 copy-start.3
  56.5 5.1 %all-to-all-done.1.second_ref = bf16[8,144,256]{2,1,0:T(8,128)(2,1)S(1)} async-done(((bf16[8,144,256]{2,1,0:T(8,128)(2,1)}), bf16[8,144,256]{2,1,0:T(8,128)(2,1)S(1)}, u32[]{:S(2)}, u32[]{:S(2)}) %all-to-all-start.1) | async-done | bytes 589856 | tf_op jit(solution)/shard_map/all_to_all | solution.py:20
  61.6 0.0 copy-start.1
  61.6 0.0 copy-done.3
  61.6 0.8 copy-done.1
  62.5 3.2 %teacher_rows.1 = bf16[96,896]{1,0:T(8,128)(2,1)} custom-call(f32[144,256]{1,0:T(8,128)} %get-tuple-element.22.keep_ref, bf16[144,256]{1,0:T(8,128)(2,1)} %copy-done.3, bf16[8,144,256]{2,1,0:T(8,128)(2,1)} %copy-done.1, bf16[144,512]{1,0:T(8,128)(2,1)} %residual_ref.1, s32[3,144]{1,0:T(4,128)} %pad_add_fusion.slots_ref, ...), custom_call_target="tpu_custom_call" | custom-call | flops 24772608 | bytes 1179648 | tf_op jit(solution)/shard_map/teacher_rows/pallas_call | solution.py:211
  65.7 29.3 %all_to_all.20 = bf16[12,8,896]{2,1,0:T(8,128)(2,1)S(1)} all-to-all(bf16[12,8,896]{2,1,0:T(8,128)(2,1)} %bitcast.14), channel_id=1, replica_groups=mesh['x_lo'=2,'z_hi'=3,'z_lo'=4,'core'=2,'x_hi'=2,'y'=8] {'z_hi','z_lo'}, dimensions={0} | all-to-all | bytes 344064 | tf_op jit(solution)/shard_map/all_to_all | solution.py:20
  95.0 8.5 %all_gather.3.rows_ref = bf16[384,896]{1,0:T(8,128)(2,1)} all-gather(bf16[96,896]{1,0:T(8,128)(2,1)S(1)} %bitcast.15), channel_id=1, replica_groups=mesh['x_lo'=2,'z_hi'=3,'z_lo'=4,'core'=2,'x_hi'=2,'y'=8] {'x_lo','core'}, dimensions={0}, use_global_device_ids=true | all-gather | bytes 860160 | tf_op jit(solution)/shard_map/all_gather | solution.py:327
  103.5 0.0 copy-done.6
  103.5 0.0 copy-done.7
  103.5 0.0 copy-done.8
  103.5 4.7 %gradient.1 = (bf16[864,512]{1,0:T(8,128)(2,1)}, f32[1,1]{1,0:T(1,128)}) custom-call(s32[1]{0:T(128)} %bitcast.refs_0_.me_ref, bf16[384,896]{1,0:T(8,128)(2,1)} %all_gather.3.rows_ref, bf16[144,1408]{1,0:T(8,128)(2,1)} %get-tuple-element.31.refs_0_, bf16[144,1408]{1,0:T(8,128)(2,1)} %copy-done.6, bf16[144,1408]{1,0:T(8,128)(2,1)} %copy-done.7, ...), custom_call_target="tpu_custom_call" | custom-call | flops 1019215872 | bytes 1990656 | tf_op jit(solution)/shard_map/gradient/pallas_call | solution.py:270
  108.1 3.7 %all-to-all-start.3 = ((bf16[12,72,512]{2,1,0:T(8,128)(2,1)}), bf16[12,72,512]{2,1,0:T(8,128)(2,1)S(1)}, u32[]{:S(2)}, u32[]{:S(2)}) async-start(bf16[12,72,512]{2,1,0:T(8,128)(2,1)} %bitcast.13), calls=%async_computation.3 | async-start | bytes 1769472 | tf_op jit(solution)/shard_map/all_to_all | solution.py:20
  111.9 3.1 %pmax.35 = f32[]{:T(128)} all-reduce(f32[]{:T(128)} %bitcast.9), channel_id=1, replica_groups=mesh['x_lo'=2,'z_hi'=3,'z_lo'=4,'core'=2,'x_hi'=2,'y'=8] {'core'}, use_global_device_ids=true, to_apply=%region_2.3 | all-reduce | flops 1 | bytes 8 | tf_op jit(solution)/shard_map/pmax | solution.py:333
  115.0 10.4 %pmax.36 = f32[]{:T(128)} all-reduce(f32[]{:T(128)} %pmax.35), channel_id=1, replica_groups=mesh['x_lo'=2,'z_hi'=3,'z_lo'=4,'core'=2,'x_hi'=2,'y'=8] {'x_hi','x_lo'}, use_global_device_ids=true, to_apply=%region_3.4 | all-reduce | flops 1 | bytes 8 | tf_op jit(solution)/shard_map/pmax | solution.py:333
  125.4 17.2 %pmax.37 = f32[]{:T(128)} all-reduce(f32[]{:T(128)} %pmax.36), channel_id=1, replica_groups=mesh['x_lo'=2,'z_hi'=3,'z_lo'=4,'core'=2,'x_hi'=2,'y'=8] {'y'}, use_global_device_ids=true, to_apply=%region_4.5 | all-reduce | flops 1 | bytes 8 | tf_op jit(solution)/shard_map/pmax | solution.py:333
  142.6 12.6 %pmax.38 = f32[]{:T(128)} all-reduce(f32[]{:T(128)} %pmax.37), channel_id=1, replica_groups=mesh['x_lo'=2,'z_hi'=3,'z_lo'=4,'core'=2,'x_hi'=2,'y'=8] {'z_lo'}, use_global_device_ids=true, to_apply=%region_5.6 | all-reduce | flops 1 | bytes 8 | tf_op jit(solution)/shard_map/pmax | solution.py:333
  155.2 11.6 %pmax.39 = f32[]{:T(128)} all-reduce(f32[]{:T(128)} %pmax.38), channel_id=1, replica_groups=mesh['x_lo'=2,'z_hi'=3,'z_lo'=4,'core'=2,'x_hi'=2,'y'=8] {'z_hi'}, use_global_device_ids=true, to_apply=%region_6.7 | all-reduce | flops 1 | bytes 8 | tf_op jit(solution)/shard_map/pmax | solution.py:333
  167.5 0.0 all-to-all-done.3
  167.5 0.1 convert_reduce_fusion
  167.6 0.7 broadcast_divide_fusion
  (3 shorter events, 0.1 us)
Async XLA Ops:
  2.8 37.6 %all-to-all-start = ((bf16[8,144,512]{2,1,0:T(8,128)(2,1)}), bf16[8,144,512]{2,1,0:T(8,128)(2,1)S(1)}, u32[]{:S(2)}, u32[]{:S(2)}) async-start(bf16[8,144,512]{2,1,0:T(8,128)(2,1)} %direct_columns.1), calls=%async_computation | async-start | bytes 2359296 | tf_op jit(solution)/shard_map/all_to_all | solution.py:20
  15.7 4.1 %copy-start.4 = (f32[3456]{0:T(1024)S(1)}, f32[3456]{0:T(1024)}, u32[]{:S(2)}) copy-start(f32[3456]{0:T(1024)} %param.7) | copy-start | bytes 41476
  17.9 15.4 %collective-permute-start = (bf16[8,144,256]{2,1,0:T(8,128)(2,1)}, bf16[8,144,256]{2,1,0:T(8,128)(2,1)S(1)}, u32[]{:S(2)}, u32[]{:S(2)}) collective-permute-start(bf16[8,144,256]{2,1,0:T(8,128)(2,1)} %away_columns.1), channel_id=1, source_target_pairs={{0,8},{8,0},{1,9},{9,1},{2,10},{10,2},{3,11},{11,3},{4,12},{12,4},... | collective-permute-start | bytes 1769480 | tf_op jit(solution)/shard_map/ppermute | solution.py:299
  25.6 28.4 %collective-permute-start.1 = (bf16[144,1408]{1,0:T(8,128)(2,1)}, bf16[144,1408]{1,0:T(8,128)(2,1)S(1)}, u32[]{:S(2)}, u32[]{:S(2)}) collective-permute-start(bf16[144,1408]{1,0:T(8,128)(2,1)} %get-tuple-element.25), channel_id=1, source_target_pairs={{0,16},{16,0},{384,400},{400,384},{1,17},{17,1},{385,401},{401,385... | collective-permute-start | bytes 1216520 | tf_op jit(solution)/shard_map/ppermute | solution.py:24
  27.5 26.5 %collective-permute-start.2 = (bf16[144,1408]{1,0:T(8,128)(2,1)}, bf16[144,1408]{1,0:T(8,128)(2,1)S(1)}, u32[]{:S(2)}, u32[]{:S(2)}) collective-permute-start(bf16[144,1408]{1,0:T(8,128)(2,1)} %get-tuple-element.26), channel_id=1, source_target_pairs={{0,384},{16,400},{384,0},{400,16},{1,385},{17,401},{385,1},{401,17... | collective-permute-start | bytes 1216520 | tf_op jit(solution)/shard_map/ppermute | solution.py:24
  29.5 15.9 %copy-start.5 = (s32[144]{0:T(256)S(1)}, s32[144]{0:T(256)}, u32[]{:S(2)}) copy-start(s32[144]{0:T(256)} %param.11) | copy-start | bytes 1732
  29.5 24.6 %collective-permute-start.3 = (bf16[144,1408]{1,0:T(8,128)(2,1)}, bf16[144,1408]{1,0:T(8,128)(2,1)S(1)}, u32[]{:S(2)}, u32[]{:S(2)}) collective-permute-start(bf16[144,1408]{1,0:T(8,128)(2,1)} %get-tuple-element.27), channel_id=1, source_target_pairs={{0,400},{16,384},{384,16},{400,0},{1,401},{17,385},{385,17},{401,1... | collective-permute-start | bytes 1216520 | tf_op jit(solution)/shard_map/ppermute | solution.py:24
  33.2 0.8 copy-start.2
  40.4 6.0 %copy-start = (bf16[8,144,512]{2,1,0:T(8,128)(2,1)}, bf16[8,144,512]{2,1,0:T(8,128)(2,1)S(1)}, u32[]{:S(2)}) copy-start(bf16[8,144,512]{2,1,0:T(8,128)(2,1)S(1)} %all-to-all-done.terms_ref) | copy-start | bytes 3538948
  40.4 21.2 %all-to-all-start.1 = ((bf16[8,144,256]{2,1,0:T(8,128)(2,1)}), bf16[8,144,256]{2,1,0:T(8,128)(2,1)S(1)}, u32[]{:S(2)}, u32[]{:S(2)}) async-start(bf16[8,144,256]{2,1,0:T(8,128)(2,1)} %pair_sum.1), calls=%async_computation.1 | async-start | bytes 1179648 | tf_op jit(solution)/shard_map/all_to_all | solution.py:20
  48.5 7.9 %collective-permute-start.4 = (bf16[144,256]{1,0:T(8,128)(2,1)}, bf16[144,256]{1,0:T(8,128)(2,1)S(1)}, u32[]{:S(2)}, u32[]{:S(2)}) collective-permute-start(bf16[144,256]{1,0:T(8,128)(2,1)} %get-tuple-element.28), channel_id=1, source_target_pairs={{0,8},{8,0},{1,9},{9,1},{2,10},{10,2},{3,11},{11,3},{4,12},{12,4},... | collective-permute-start | bytes 221192 | tf_op jit(solution)/shard_map/ppermute | solution.py:307
  54.1 49.4 %copy-start.6 = (bf16[144,1408]{1,0:T(8,128)(2,1)}, bf16[144,1408]{1,0:T(8,128)(2,1)S(1)}, u32[]{:S(2)}) copy-start(bf16[144,1408]{1,0:T(8,128)(2,1)S(1)} %collective-permute-done.1.refs_1_) | copy-start | bytes 1216516
  54.1 49.4 %copy-start.7 = (bf16[144,1408]{1,0:T(8,128)(2,1)}, bf16[144,1408]{1,0:T(8,128)(2,1)S(1)}, u32[]{:S(2)}) copy-start(bf16[144,1408]{1,0:T(8,128)(2,1)S(1)} %collective-permute-done.2.refs_2_) | copy-start | bytes 1216516
  54.1 49.4 %copy-start.8 = (bf16[144,1408]{1,0:T(8,128)(2,1)}, bf16[144,1408]{1,0:T(8,128)(2,1)S(1)}, u32[]{:S(2)}) copy-start(bf16[144,1408]{1,0:T(8,128)(2,1)S(1)} %collective-permute-done.3.refs_3_) | copy-start | bytes 1216516
  56.5 5.1 %copy-start.3 = (bf16[144,256]{1,0:T(8,128)(2,1)}, bf16[144,256]{1,0:T(8,128)(2,1)S(1)}, u32[]{:S(2)}) copy-start(bf16[144,256]{1,0:T(8,128)(2,1)S(1)} %collective-permute-done.4.got_ref) | copy-start | bytes 221188
  61.6 0.8 copy-start.1
  108.1 59.3 %all-to-all-start.3 = ((bf16[12,72,512]{2,1,0:T(8,128)(2,1)}), bf16[12,72,512]{2,1,0:T(8,128)(2,1)S(1)}, u32[]{:S(2)}, u32[]{:S(2)}) async-start(bf16[12,72,512]{2,1,0:T(8,128)(2,1)} %bitcast.13), calls=%async_computation.3 | async-start | bytes 1769472 | tf_op jit(solution)/shard_map/all_to_all | solution.py:20
